TPU v7x, 32 devices: a whole 2x2x4 slice. The times are simulated.
32 devices in a mesh: expert: 4 (over y, x), tensor: 4 (over z), rep: 2 (over core).
Axes of the slice: x: 2, y: 2, z: 4, core: 2. Of those that a mesh axis runs over, the one named last changes fastest.
Arguments:
- requests: bfloat16 [512, 1536], P('expert', ('tensor', 'rep')), may hold values from -6 to 6
- expert_ids: int32 [512, 2], P('expert'), may hold values from 0 to 3, all different within a row; in each aligned block of 128 rows (0 to 127, 128 to 255, ...) at most 96 rows name the same one
- gate_values: float32 [512, 2], P('expert'), may hold values from 0.2 to 1
- w_up: bfloat16 [4, 1536, 6144], P(None, 'expert', ('tensor', 'rep')), may hold values from -0.15625 to 0.15625
- w_down: bfloat16 [4, 1536, 6144], P(None, 'expert', ('tensor', 'rep')), may hold values from -0.078125 to 0.078125
- tower_in: bfloat16 [1536, 768], P(('tensor', 'rep')), may hold values from -0.15625 to 0.15625
- tower_bias: float32 [768], replicated, may hold values from -3 to 3
- tower_out: float32 [3, 256], replicated, may hold values from -0.375 to 0.375
- out_bias: float32 [3], replicated, may hold values from -3 to 3
Outputs:
- mixed: bfloat16 [512, 1536], P('expert', ('tensor', 'rep'))
- scores: float32 [3, 512], P(None, ('expert', 'tensor', 'rep'))
Inputs may be any that keep to these rules, and one draw needn't show every extreme that they name: `expert_ids`: each row names two different experts. In the rows of one device (128 requests) no expert is named more than 96 times, a bound that some block reaches.
All inputs are finite; a program needn't handle non-finite values.
Results may differ from a plain program's by a relative error of at most 0.015.
Values may be sent and summed in bfloat16 or wider, within the bound.
No kernel may reach another device: no remote copies, remote signals or barrier semaphores. Data moves between devices by JAX's collectives and lax.ppermute only.
A program may use at most 64 MiB of HBM per device.

v0:
```python
import jax
import jax.numpy as jnp
from jax import lax
from jax.sharding import PartitionSpec as P


def tower_head(pre, tower_bias, tower_out, out_bias):
    active = jax.nn.relu(pre + tower_bias[None, :])
    active = active.reshape(pre.shape[0], tower_out.shape[0], tower_out.shape[1])
    logits = jnp.sum(active * tower_out[None, :, :], axis=2) + out_bias[None, :]
    return jax.nn.sigmoid(logits).T


def per_device(
    requests, expert_ids, gate_values, w_up, w_down, tower_in, tower_bias, tower_out, out_bias
):
    groups = lax.axis_size("expert")
    experts = w_up.shape[0]
    local_experts = experts // groups
    tok_rows = requests.shape[0]
    capacity = 3 * tok_rows // experts
    serve_up, serve_down = (
        lax.all_to_all(w_up, "expert", split_axis=0, concat_axis=1, tiled=True),
        lax.all_to_all(w_down, "expert", split_axis=0, concat_axis=1, tiled=True),
    )
    flat_ids = expert_ids.reshape(-1)
    onehot = (flat_ids[:, None] == jnp.arange(experts, dtype=jnp.int32)[None, :]).astype(jnp.int32)
    before = jnp.cumsum(onehot, axis=0) - onehot
    slot_rank = jnp.sum(before * onehot, axis=1)
    slots = (flat_ids * capacity + slot_rank).reshape(tok_rows, 2)
    slot_index = jnp.arange(experts * capacity, dtype=jnp.int32)
    spread = (
        (slot_index[:, None] == slots[None, :, 0]) | (slot_index[:, None] == slots[None, :, 1])
    ).astype(jnp.bfloat16)
    full_rows = lax.all_gather(requests, ("tensor", "rep"), axis=1, tiled=True)
    outgoing = jnp.dot(spread, full_rows, preferred_element_type=jnp.float32).astype(jnp.bfloat16)
    incoming = lax.all_to_all(outgoing, "expert", split_axis=0, concat_axis=0, tiled=True)
    shaped = incoming.reshape(groups, local_experts, capacity, incoming.shape[1])
    hidden_pre = jnp.einsum("secd,edh->sech", shaped, serve_up, preferred_element_type=jnp.float32)
    hidden = jax.nn.relu(hidden_pre).astype(jnp.bfloat16)
    partial_value = jnp.einsum(
        "sech,edh->secd", hidden, serve_down, preferred_element_type=jnp.float32
    )
    summed = lax.psum_scatter(
        partial_value.astype(jnp.bfloat16), ("tensor", "rep"), scatter_dimension=3, tiled=True
    ).astype(jnp.float32)
    expert_out = summed.astype(jnp.bfloat16).reshape(
        groups * local_experts * capacity, summed.shape[3]
    )
    returned = lax.all_to_all(expert_out, "expert", split_axis=0, concat_axis=0, tiled=True)
    pick_first = (slots[:, 0:1] == slot_index[None, :]).astype(jnp.bfloat16)
    pick_second = (slots[:, 1:2] == slot_index[None, :]).astype(jnp.bfloat16)
    first = jnp.dot(pick_first, returned, preferred_element_type=jnp.float32)
    second = jnp.dot(pick_second, returned, preferred_element_type=jnp.float32)
    mixed = (gate_values[:, 0:1] * first + gate_values[:, 1:2] * second).astype(jnp.bfloat16)
    pre = lax.psum_scatter(
        jnp.dot(mixed, tower_in, preferred_element_type=jnp.float32).astype(jnp.bfloat16),
        ("tensor", "rep"),
        scatter_dimension=0,
        tiled=True,
    ).astype(jnp.float32)
    scores = tower_head(pre, tower_bias, tower_out, out_bias)
    return (mixed, scores)


def solution(mesh):
    in_specs = (
        P("expert", ("tensor", "rep")),
        P("expert", None),
        P("expert", None),
        P(None, "expert", ("tensor", "rep")),
        P(None, "expert", ("tensor", "rep")),
        P(("tensor", "rep"), None),
        P(),
        P(),
        P(),
    )
    out_specs = (P("expert", ("tensor", "rep")), P(None, ("expert", "tensor", "rep")))
    return jax.shard_map(
        per_device, mesh=mesh, in_specs=in_specs, out_specs=out_specs, check_vma=False
    )
```

profile of v0, /device:TPU:0, one launch (start us, length us, event | category | flops | bytes accessed | tf_op | source)
XLA Modules:
  0.0 198.6 jit_solution(8744839714044765721)
XLA Ops:
  7.2 0.8 copy.32
  8.2 0.1 eq.81
  8.3 1.2 reduce-window.6
  10.0 0.1 reduce_sum.21
  10.2 0.7 multiply_add_fusion
  10.9 16.4 %all_gather.3 = bf16[128,1536]{0,1:T(8,128)(2,1)S(1)} all-gather(bf16[128,192]{0,1:T(8,128)(2,1)} %param.9), channel_id=1, replica_groups=mesh['expert'=4,'tensor'=4,'rep'=2] {'tensor','rep'}, dimensions={1}, use_global_device_ids=true | all-gather | bytes 442368 | tf_op jit(solution)/shard_map/all_gather | solution.py:35
  27.3 0.5 convolution_convert_fusion
  27.8 19.8 %all_to_all.39 = bf16[4,96,1536]{2,1,0:T(8,128)(2,1)} all-to-all(bf16[4,96,1536]{2,1,0:T(8,128)(2,1)S(1)} %bitcast.56), channel_id=1, replica_groups=mesh['expert'=4,'tensor'=4,'rep'=2] {'expert'}, dimensions={0} | all-to-all | bytes 2359296 | tf_op jit(solution)/shard_map/all_to_all | solution.py:37
  47.6 30.1 %all_to_all.40 = bf16[4,384,768]{2,1,0:T(8,128)(2,1)S(1)} all-to-all(bf16[4,384,768]{2,1,0:T(8,128)(2,1)S(1)} %copy-done.1), channel_id=1, replica_groups=mesh['expert'=4,'tensor'=4,'rep'=2] {'expert'}, dimensions={0} | all-to-all | bytes 4718592 | tf_op jit(solution)/shard_map/all_to_all | solution.py:23
  77.7 29.5 %all_to_all.41 = bf16[4,384,768]{2,1,0:T(8,128)(2,1)} all-to-all(bf16[4,384,768]{2,1,0:T(8,128)(2,1)S(1)} %copy-done.2), channel_id=1, replica_groups=mesh['expert'=4,'tensor'=4,'rep'=2] {'expert'}, dimensions={0} | all-to-all | bytes 4718592 | tf_op jit(solution)/shard_map/all_to_all | solution.py:24
  107.3 5.5 %fusion = bf16[4,1,96,1536]{3,2,0,1:T(8,128)(2,1)} fusion(bf16[1536,768,1]{1,0,2:T(8,128)(2,1)} %bitcast.58, bf16[4,96,1536]{2,1,0:T(8,128)(2,1)} %all_to_all.39, bf16[1536,768,1]{1,0,2:T(8,128)(2,1)S(1)} %bitcast.57), kind=kOutput, calls=%fused_computation.2 | convolution fusion | flops 1813118976 | bytes 7077888 | tf_op jit(solution)/shard_map/sech,edh->secd/dot_general | solution.py:41
  112.7 2.6 %copy.38 = bf16[4,1,96,1536]{2,0,1,3:T(4,128)(2,1)S(1)} copy(bf16[4,1,96,1536]{3,2,0,1:T(8,128)(2,1)} %fusion) | data formatting | bytes 2359296
  115.4 1.9 reshape.69
  117.3 32.7 %reduce-scatter.7.cloned.1.call-done = bf16[192,384]{1,0:T(8,128)(2,1)} async-done(((bf16[1536,384]{1,0:T(8,128)(2,1)}), bf16[192,384]{1,0:T(8,128)(2,1)}) %reduce-scatter.7.cloned.1.call-update) | async-done | bytes 147472
  150.0 1.1 reshape.70
  151.0 0.8 copy.39
  151.9 3.6 %all-to-all-start.3 = ((bf16[4,96,192]{2,1,0:T(8,128)(2,1)}), bf16[4,96,192]{2,1,0:T(8,128)(2,1)S(1)}, u32[]{:S(2)}, u32[]{:S(2)}) async-start(bf16[4,96,192]{2,1,0:T(8,128)(2,1)} %bitcast.13), calls=%async_computation.3 | async-start | bytes 393216 | tf_op jit(solution)/shard_map/all_to_all | solution.py:50
  155.5 5.2 %all-to-all-done.3 = bf16[4,96,192]{2,1,0:T(8,128)(2,1)S(1)} async-done(((bf16[4,96,192]{2,1,0:T(8,128)(2,1)}), bf16[4,96,192]{2,1,0:T(8,128)(2,1)S(1)}, u32[]{:S(2)}, u32[]{:S(2)}) %all-to-all-start.3) | async-done | bytes 147488 | tf_op jit(solution)/shard_map/all_to_all | solution.py:50
  160.7 0.3 convolution_multiply_fusion
  161.0 0.3 fusion.3
  161.3 0.9 convolution_convert_fusion.2
  162.2 27.9 %reduce-scatter.5.cloned.1.call-done = bf16[16,768]{1,0:T(8,128)(2,1)} async-done(((bf16[128,768]{1,0:T(8,128)(2,1)}), bf16[16,768]{1,0:T(8,128)(2,1)}) %reduce-scatter.5.cloned.1.call-update) | async-done | bytes 24592 | tf_op jit(solution)/shard_map/reduce_scatter | solution.py:56
  190.2 0.7 add_maximum_fusion
  191.1 0.7 copy.37
  (35 shorter events, 0.9 us)
Async XLA Ops:
  7.2 154.1 %copy-start = (bf16[192,768]{1,0:T(8,128)(2,1)S(1)}, bf16[192,768]{1,0:T(8,128)(2,1)}, u32[]{:S(2)}) copy-start(bf16[192,768]{1,0:T(8,128)(2,1)} %param.14) | copy-start | bytes 884740
  7.2 142.8 %reduce-scatter.7.cloned.1.call-start = ((), (), s32[]{:S(2)}) async-start(), calls=%async_computation.7 | async-start | bytes 1327104
  27.8 19.8 %copy-start.1 = (bf16[4,384,768]{2,1,0:T(8,128)(2,1)S(1)}, bf16[4,384,768]{2,1,0:T(8,128)(2,1)}, u32[]{:S(2)}) copy-start(bf16[4,384,768]{2,1,0:T(8,128)(2,1)} %param.12) | copy-start | bytes 7077892
  47.6 30.1 %copy-start.2 = (bf16[4,384,768]{2,1,0:T(8,128)(2,1)S(1)}, bf16[4,384,768]{2,1,0:T(8,128)(2,1)}, u32[]{:S(2)}) copy-start(bf16[4,384,768]{2,1,0:T(8,128)(2,1)} %param.13) | copy-start | bytes 7077892
  117.3 38.2 %copy-start.6 = (f32[128,2]{0,1:T(2,128)S(1)}, f32[128,2]{0,1:T(2,128)}, u32[]{:S(2)}) copy-start(f32[128,2]{0,1:T(2,128)} %param.11) | copy-start | bytes 3076
  117.3 72.9 %copy-start.4 = (f32[768]{0:T(1024)S(1)}, f32[768]{0:T(1024)}, u32[]{:S(2)}) copy-start(f32[768]{0:T(1024)} %param.15) | copy-start | bytes 9220
  117.3 73.7 %copy-start.5 = (f32[3,256]{1,0:T(4,128)S(1)}, f32[3,256]{1,0:T(4,128)}, u32[]{:S(2)}) copy-start(f32[3,256]{1,0:T(4,128)} %param.16) | copy-start | bytes 9220
  117.3 73.7 %copy-start.7 = (f32[3]{0:T(128)S(1)}, f32[3]{0:T(128)}, u32[]{:S(2)}) copy-start(f32[3]{0:T(128)} %param.17) | copy-start | bytes 40
  151.9 8.8 %all-to-all-start.3 = ((bf16[4,96,192]{2,1,0:T(8,128)(2,1)}), bf16[4,96,192]{2,1,0:T(8,128)(2,1)S(1)}, u32[]{:S(2)}, u32[]{:S(2)}) async-start(bf16[4,96,192]{2,1,0:T(8,128)(2,1)} %bitcast.13), calls=%async_computation.3 | async-start | bytes 393216 | tf_op jit(solution)/shard_map/all_to_all | solution.py:50
  155.5 34.7 %reduce-scatter.5.cloned.1.call-start = ((), (), s32[]{:S(2)}) async-start(), calls=%async_computation.6 | async-start | bytes 221184 | tf_op jit(solution)/shard_map/reduce_scatter | solution.py:56
  161.3 30.5 %copy-start.3 = (bf16[128,192]{0,1:T(8,128)(2,1)}, bf16[128,192]{0,1:T(8,128)(2,1)S(1)}, u32[]{:S(2)}) copy-start(bf16[128,192]{0,1:T(8,128)(2,1)S(1)} %fusion.3) | copy-start | bytes 147460
Sparse Core Ops, SparseCore 0:
  117.4 32.5 reduce-scatter.6
  162.4 27.7 reduce-scatter.4
where the time goes:
time: 199 us
  blocking collectives  95.8 us (48%)
  waiting for transfers between devices  65.8 us (33%)
  between operations  14.2 us (7%)
  local copies, waits for them, and re-layouts  8.73 us (4%)
  matrix products  7.42 us (4%)
  starting transfers between devices  3.68 us (2%)
  other arithmetic  2.92 us (1%)
    unnamed x3, waiting for transfers between devices  32.7 us
    all_to_all x1, blocking collectives, per_device(): lax.all_to_all(w_up, 'expert', split_axis=0, concat_axis=1, tiled=True)  30.1 us
    all_to_all x1, blocking collectives, per_device(): lax.all_to_all(w_down, 'expert', split_axis=0, concat_axis=1, tiled=True)  29.5 us
    reduce_scatter x1, waiting for transfers between devices, per_device(): lax.psum_scatter(jnp.dot(mixed, tower_in, preferred_element_type=jnp.floa...  27.9 us
    all_to_all x1, blocking collectives, per_device(): lax.all_to_all(outgoing, 'expert', split_axis=0, concat_axis=0, tiled=True)  19.8 us
    all_gather x1, blocking collectives, per_device(): full_rows = lax.all_gather(requests, ('tensor', 'rep'), axis=1, tiled=True)  16.4 us
    unnamed x22, local copies, waits for them, and re-layouts  7.94 us
    dot_general x1, matrix products, per_device(): jnp.einsum('sech,edh->secd', hidden, serve_down, preferred_element_type=j...  5.47 us
  transfers between devices with their start and end apart: 3, of which 3 were waited for; matrix products, arithmetic and copies ran while one was open for 0% of the time, Pallas kernels for 0%

commit v1 on v0

--- a/solution.py
+++ b/solution.py
@@ -1,7 +1,13 @@
 import jax
 import jax.numpy as jnp
 from jax import lax
+from jax.experimental import pallas as pl
+from jax.experimental.pallas import tpu as pltpu
 from jax.sharding import PartitionSpec as P
+
+ALL = ("expert", "tensor", "rep")
+F32 = jnp.float32
+BF16 = jnp.bfloat16
 
 
 def tower_head(pre, tower_bias, tower_out, out_bias):
@@ -11,7 +17,7 @@
     return jax.nn.sigmoid(logits).T
 
 
-def per_device(
+def moved_weights(
     requests, expert_ids, gate_values, w_up, w_down, tower_in, tower_bias, tower_out, out_bias
 ):
     groups = lax.axis_size("expert")
@@ -63,7 +69,191 @@
     return (mixed, scores)
 
 
+def permute(x, move):
+    sizes = [lax.axis_size(a) for a in ALL]
+    pairs = []
+    for e in range(sizes[0]):
+        for t in range(sizes[1]):
+            for r in range(sizes[2]):
+                e2, t2, r2 = move(e, t, r)
+                pairs.append(
+                    ((e * sizes[1] + t) * sizes[2] + r, (e2 * sizes[1] + t2) * sizes[2] + r2)
+                )
+    return lax.ppermute(x, ALL, pairs)
+
+
+def gather_cols(packed, width):
+    tail = packed[:, width:].astype(F32)
+    ids = [tail[:, k : k + 1] for k in range(2)]
+    gates = [
+        tail[:, 2 + 3 * k : 3 + 3 * k]
+        + tail[:, 3 + 3 * k : 4 + 3 * k]
+        + tail[:, 4 + 3 * k : 5 + 3 * k]
+        for k in range(2)
+    ]
+    return ids, gates
+
+
+def up_kernel(place_ref, own_ref, other_ref, w_ref, *rest, width, blocks):
+    outs, (xo_ref, xp_ref) = rest[:-2], rest[-2:]
+    tok = own_ref.shape[1]
+    experts, _, hid = w_ref.shape
+    flip = place_ref[0]
+    r = place_ref[1]
+    for m in range(blocks):
+        src = jnp.bitwise_xor(flip, m)
+        xo_ref[m * tok : (m + 1) * tok, :] = own_ref[src]
+        xp_ref[m * tok : (m + 1) * tok, :] = other_ref[src]
+    ids, _ = gather_cols(xo_ref[...], width)
+    xo = xo_ref[:, :width]
+    xp = xp_ref[:, :width]
+    tile = 256
+    for n in range(0, hid, tile):
+        parts = []
+        for j in range(experts):
+            wo = w_ref[j, pl.ds(pl.multiple_of(r * width, width), width), n : n + tile]
+            wp = w_ref[j, pl.ds(pl.multiple_of((1 - r) * width, width), width), n : n + tile]
+            parts.append(
+                jnp.dot(xo, wo, preferred_element_type=F32)
+                + jnp.dot(xp, wp, preferred_element_type=F32)
+            )
+        for k in range(2):
+            acc = parts[experts - 1]
+            for j in range(experts - 1):
+                acc = jnp.where(ids[k] == float(j), parts[j], acc)
+            acc = acc.astype(BF16)
+            for m in range(blocks):
+                outs[k * blocks + m][:, n : n + tile] = acc[m * tok : (m + 1) * tok, :]
+
+
+def down_kernel(place_ref, own_ref, w_ref, *rest, width, blocks):
+    hidden, (keep_ref, send_ref, y_ref) = rest[: 2 * blocks], rest[2 * blocks :]
+    tok = own_ref.shape[1]
+    experts = w_ref.shape[0]
+    flip = place_ref[0]
+    r = place_ref[1]
+    packed = jnp.concatenate([own_ref[jnp.bitwise_xor(flip, m)] for m in range(blocks)], axis=0)
+    ids, gates = gather_cols(packed, width)
+    h = [
+        jnp.concatenate([hidden[k * blocks + m][...] for m in range(blocks)], axis=0)
+        for k in range(2)
+    ]
+    zero = jnp.zeros_like(h[0])
+    keep = send = None
+    for j in range(experts):
+        hit = [ids[k] == float(j) for k in range(2)]
+        rows = jnp.where(hit[0], h[0], jnp.where(hit[1], h[1], zero))
+        gate = jnp.where(hit[0], gates[0], jnp.where(hit[1], gates[1], 0.0))
+        nt = (((1,), (1,)), ((), ()))
+        wk = w_ref[j, pl.ds(pl.multiple_of(r * width, width), width), :]
+        ws = w_ref[j, pl.ds(pl.multiple_of((1 - r) * width, width), width), :]
+        a = gate * lax.dot_general(rows, wk, nt, preferred_element_type=F32)
+        b = gate * lax.dot_general(rows, ws, nt, preferred_element_type=F32)
+        keep = a if keep is None else keep + a
+        send = b if send is None else send + b
+    for m in range(blocks):
+        dst = jnp.bitwise_xor(flip, m)
+        keep_ref[dst] = keep[m * tok : (m + 1) * tok, :].astype(BF16)
+        send_ref[dst] = send[m * tok : (m + 1) * tok, :].astype(BF16)
+
+
+VMEM = pl.BlockSpec(memory_space=pltpu.VMEM)
+SMEM = pl.BlockSpec(memory_space=pltpu.SMEM)
+
+
+def stationary(
+    requests, expert_ids, gate_values, w_up, w_down, tower_in, tower_bias, tower_out, out_bias
+):
+    blocks = lax.axis_size("expert")
+    tok, width = requests.shape
+    hid = w_up.shape[2]
+    e, t, r = (lax.axis_index(a) for a in ALL)
+    place = jnp.stack([jnp.bitwise_xor(e, t), r]).astype(jnp.int32)
+
+    def x_of(v):
+        return permute(v, lambda e, t, r: (e ^ 1, t, r))
+
+    def y_of(v):
+        return permute(v, lambda e, t, r: (e ^ 2, t, r))
+
+    def r_of(v):
+        return permute(v, lambda e, t, r: (e, t, 1 - r))
+
+    high = gate_values.astype(BF16)
+    left = gate_values - high.astype(F32)
+    mid = left.astype(BF16)
+    low = (left - mid.astype(F32)).astype(BF16)
+    cols = [requests, expert_ids.astype(BF16)]
+    for k in range(2):
+        cols += [v[:, k : k + 1] for v in (high, mid, low)]
+    packed = jnp.concatenate(cols, axis=1)
+    own = jnp.stack(
+        [permute(packed, lambda e, t, r, k=k: (t, e ^ k, r)) for k in range(blocks)]
+    )
+    other = r_of(own)
+
+    piece = jax.ShapeDtypeStruct((tok, hid), BF16)
+    parts = pl.pallas_call(
+        lambda *refs: up_kernel(*refs, width=width, blocks=blocks),
+        out_shape=[piece] * (2 * blocks),
+        in_specs=[SMEM, VMEM, VMEM, VMEM],
+        out_specs=[VMEM] * (2 * blocks),
+        scratch_shapes=[pltpu.VMEM((blocks * tok, packed.shape[1]), BF16)] * 2,
+        name="up",
+    )(place, own, other, w_up)
+    (ao, an, ay, ad), (bo, bx, bn, bd) = parts[:blocks], parts[blocks:]
+
+    rad, rbd = x_of(ad), y_of(bd)
+    ran, rbn = x_of(an), y_of(bn)
+    fa = (ay.astype(F32) + rad.astype(F32)).astype(BF16)
+    fb = (bx.astype(F32) + rbd.astype(F32)).astype(BF16)
+    ra2, rb2 = y_of(fa), x_of(fb)
+    ha = jax.nn.relu(ao.astype(F32) + ran.astype(F32) + ra2.astype(F32)).astype(BF16)
+    hb = jax.nn.relu(bo.astype(F32) + rbn.astype(F32) + rb2.astype(F32)).astype(BF16)
+
+    hax, hay = x_of(ha), y_of(ha)
+    hbx, hby = x_of(hb), y_of(hb)
+    haxy, hbxy = x_of(hay), y_of(hbx)
+
+    piece = jax.ShapeDtypeStruct((blocks, tok, width), BF16)
+    keep, send = pl.pallas_call(
+        lambda *refs: down_kernel(*refs, None, width=width, blocks=blocks),
+        out_shape=[piece] * 2,
+        in_specs=[SMEM] + [VMEM] * (2 + 2 * blocks),
+        out_specs=[VMEM] * 2,
+        name="down",
+    )(place, own, w_down, ha, hax, hay, haxy, hb, hbx, hby, hbxy)
+
+    back = r_of(send)
+    both = (keep.astype(F32) + back.astype(F32)).astype(BF16)
+    got = [permute(both[k], lambda e, t, r, k=k: (t ^ k, e, r)) for k in range(blocks)]
+    mixed = sum(v.astype(F32) for v in got).astype(BF16)
+
+    pre = jnp.dot(mixed, tower_in, preferred_element_type=F32).astype(BF16)
+    reps = lax.axis_size("rep")
+    pre = pre.reshape(blocks, reps, tok // blocks // reps, pre.shape[1])
+    mine = lax.dynamic_index_in_dim(pre, r, 1, keepdims=False)
+    theirs = lax.dynamic_index_in_dim(pre, 1 - r, 1, keepdims=False)
+    half = (mine.astype(F32) + r_of(theirs).astype(F32)).astype(BF16)
+    total = lax.dynamic_index_in_dim(half, t, 0, keepdims=False).astype(F32)
+    for k in range(1, blocks):
+        out = lax.dynamic_index_in_dim(half, jnp.bitwise_xor(t, k), 0, keepdims=False)
+        total = total + permute(out, lambda e, t, r, k=k: (e, t ^ k, r)).astype(F32)
+    scores = tower_head(total, tower_bias, tower_out, out_bias)
+    return (mixed, scores)
+
+
 def solution(mesh):
+    groups, n_tensor, n_rep = (mesh.shape[a] for a in ALL)
+
+    def per_device(*args):
+        requests, w_up = args[0], args[3]
+        rows = 2 * groups * requests.shape[0]
+        fits = groups == n_tensor and groups == 2 * 2 and n_rep == 2 and w_up.shape[0] <= 256
+        if fits and rows <= requests.shape[1] * n_tensor * n_rep:
+            return stationary(*args)
+        return moved_weights(*args)
+
     in_specs = (
         P("expert", ("tensor", "rep")),
         P("expert", None),

time: 199 us -> 106 us (0.53)
  blocking collectives: 95.8 us -> 0 us
  starting transfers between devices: 3.68 us -> 38.6 us
  waiting for transfers between devices: 65.8 us -> 42.6 us
  between operations: 14.2 us -> 0.94 us
  Pallas kernels: 0 us -> 10.1 us
  matrix products: 7.42 us -> 0.21 us
  other arithmetic: 2.92 us -> 7.35 us
  local copies, waits for them, and re-layouts: 8.73 us -> 5.53 us
    all_to_all x3 -> x0, blocking collectives: 79.4 us -> none  [the longest x1 30.1 us: per_device(): lax.all_to_all(w_up, 'expert', split_axis=0, concat_axis=1, tiled=True)]
    ppermute x0 -> x26, waiting for transfers between devices: none -> 42.6 us  [permute(): return lax.ppermute(x, ALL, pairs)]
    ppermute x0 -> x26, starting transfers between devices: none -> 38.6 us  [permute(): return lax.ppermute(x, ALL, pairs)]
    unnamed x3 -> x0, waiting for transfers between devices: 32.7 us -> none
    reduce_scatter x1 -> x0, waiting for transfers between devices: 27.9 us -> none  [per_device(): lax.psum_scatter(jnp.dot(mixed, tower_in, preferred_element_type=jnp.floa...]
    all_gather x1 -> x0, blocking collectives: 16.4 us -> none  [per_device(): full_rows = lax.all_gather(requests, ('tensor', 'rep'), axis=1, tiled=True)]
    pallas_call x0 -> x2, Pallas kernels: none -> 10.1 us  [the longest x1 5.22 us: stationary(): pl.pallas_call(lambda *refs: down_kernel(*refs, None, width=width, blocks...]
    dot_general x5 -> x1, matrix products: 7.42 us -> 0.21 us  [stationary(): pre = jnp.dot(mixed, tower_in, preferred_element_type=F32).astype(BF16)]
  transfers between devices with their start and end apart: 3 -> 26, of which waited for: 3 -> 14; matrix products, arithmetic and copies ran while one was open for 0% -> 5% of each run, Pallas kernels for 0% -> 0%
where the time goes in v1:
time: 106 us; the launch traced here: 105 us
  waiting for transfers between devices  42.6 us (40%)
  starting transfers between devices  38.6 us (36%)
  Pallas kernels  10.1 us (10%)
  other arithmetic  7.35 us (7%)
  local copies, waits for them, and re-layouts  5.53 us (5%)
    ppermute x26, waiting for transfers between devices, permute(): return lax.ppermute(x, ALL, pairs)  42.6 us
    ppermute x26, starting transfers between devices, permute(): return lax.ppermute(x, ALL, pairs)  38.6 us
    pallas_call x1, Pallas kernels, stationary(): pl.pallas_call(lambda *refs: down_kernel(*refs, None, width=width, blocks...  5.22 us
    pallas_call x1, Pallas kernels, stationary(): pl.pallas_call(lambda *refs: up_kernel(*refs, width=width, blocks=blocks)...  4.86 us
    unnamed x31, local copies, waits for them, and re-layouts  4.34 us
  transfers between devices with their start and end apart: 26, of which 14 were waited for; matrix products, arithmetic and copies ran while one was open for 5% of the time, Pallas kernels for 0%

profile of v1, /device:TPU:0, one launch (start us, length us, event | category | flops | bytes accessed | tf_op | source)
XLA Modules:
  0.0 105.3 jit_solution(9579014258363599943)
XLA Ops:
  4.8 5.7 %collective-permute-start.1 = (bf16[128,200]{1,0:T(8,128)(2,1)S(1)}, bf16[128,200]{1,0:T(8,128)(2,1)S(1)}, u32[]{:S(2)}, u32[]{:S(2)}) collective-permute-start(bf16[128,200]{1,0:T(8,128)(2,1)S(1)} %concatenate.3), channel_id=1, source_target_pairs={{0,2},{1,3},{2,10},{3,11},{4,18},{5,19},{6,26},{7,27},{8,0},{9,1},... | collective-permute-start | bytes 153608 | tf_op jit(solution)/shard_map/ppermute | solution.py:82
  10.5 3.5 %collective-permute-start.2 = (bf16[128,200]{1,0:T(8,128)(2,1)S(1)}, bf16[128,200]{1,0:T(8,128)(2,1)S(1)}, u32[]{:S(2)}, u32[]{:S(2)}) collective-permute-start(bf16[128,200]{1,0:T(8,128)(2,1)S(1)} %concatenate.3), channel_id=1, source_target_pairs={{0,4},{1,5},{2,12},{3,13},{4,20},{5,21},{6,28},{7,29},{8,6},{9,7},... | collective-permute-start | bytes 153608 | tf_op jit(solution)/shard_map/ppermute | solution.py:82
  14.0 1.9 %collective-permute-start.3 = (bf16[128,200]{1,0:T(8,128)(2,1)S(1)}, bf16[128,200]{1,0:T(8,128)(2,1)S(1)}, u32[]{:S(2)}, u32[]{:S(2)}) collective-permute-start(bf16[128,200]{1,0:T(8,128)(2,1)S(1)} %concatenate.3), channel_id=1, source_target_pairs={{0,6},{1,7},{2,14},{3,15},{4,22},{5,23},{6,30},{7,31},{8,4},{9,5},... | collective-permute-start | bytes 153608 | tf_op jit(solution)/shard_map/ppermute | solution.py:82
  15.9 1.8 %collective-permute-done.2 = bf16[128,200]{1,0:T(8,128)(2,1)S(1)} collective-permute-done((bf16[128,200]{1,0:T(8,128)(2,1)S(1)}, bf16[128,200]{1,0:T(8,128)(2,1)S(1)}, u32[]{:S(2)}, u32[]{:S(2)}) %collective-permute-start.2) | collective-permute-done | bytes 51232 | tf_op jit(solution)/shard_map/ppermute | solution.py:82
  17.7 1.5 %collective-permute-done.3 = bf16[128,200]{1,0:T(8,128)(2,1)S(1)} collective-permute-done((bf16[128,200]{1,0:T(8,128)(2,1)S(1)}, bf16[128,200]{1,0:T(8,128)(2,1)S(1)}, u32[]{:S(2)}, u32[]{:S(2)}) %collective-permute-start.3) | collective-permute-done | bytes 51232 | tf_op jit(solution)/shard_map/ppermute | solution.py:82
  21.6 4.9 %up.1 = (bf16[128,768]{1,0:T(8,128)(2,1)}, bf16[128,768]{1,0:T(8,128)(2,1)}, bf16[128,768]{1,0:T(8,128)(2,1)}, bf16[128,768]{1,0:T(8,128)(2,1)}, bf16[128,768]{1...) custom-call(s32[2]{0:T(128)} %pad_add_fusion.refs_0_, ...), custom_call_target="tpu_custom_call" | custom-call | tf_op jit(solution)/shard_map/up/pallas_call | solution.py:196
  26.4 3.4 %collective-permute-start.12 = (bf16[128,768]{1,0:T(8,128)(2,1)}, bf16[128,768]{1,0:T(8,128)(2,1)S(1)}, u32[]{:S(2)}, u32[]{:S(2)}) collective-permute-start(bf16[128,768]{1,0:T(8,128)(2,1)} %get-tuple-element.19), channel_id=1, source_target_pairs={{0,16},{1,17},{2,18},{3,19},{4,20},{5,21},{6,22},{7,23},{8,24},{9,... | collective-permute-start | bytes 589832 | tf_op jit(solution)/shard_map/ppermute | solution.py:82
  29.8 2.7 %collective-permute-start.6 = (bf16[128,768]{1,0:T(8,128)(2,1)}, bf16[128,768]{1,0:T(8,128)(2,1)S(1)}, u32[]{:S(2)}, u32[]{:S(2)}) collective-permute-start(bf16[128,768]{1,0:T(8,128)(2,1)} %get-tuple-element.15), channel_id=1, source_target_pairs={{0,8},{1,9},{2,10},{3,11},{4,12},{5,13},{6,14},{7,15},{8,0},{9,1},... | collective-permute-start | bytes 589832 | tf_op jit(solution)/shard_map/ppermute | solution.py:82
  32.6 3.2 %collective-permute-done.12 = bf16[128,768]{1,0:T(8,128)(2,1)S(1)} collective-permute-done((bf16[128,768]{1,0:T(8,128)(2,1)}, bf16[128,768]{1,0:T(8,128)(2,1)S(1)}, u32[]{:S(2)}, u32[]{:S(2)}) %collective-permute-start.12) | collective-permute-done | bytes 196640 | tf_op jit(solution)/shard_map/ppermute | solution.py:82
  36.7 2.8 %collective-permute-start.13 = (bf16[128,768]{1,0:T(8,128)(2,1)S(1)}, bf16[128,768]{1,0:T(8,128)(2,1)S(1)}, u32[]{:S(2)}, u32[]{:S(2)}) collective-permute-start(bf16[128,768]{1,0:T(8,128)(2,1)S(1)} %add_convert_fusion.1), channel_id=1, source_target_pairs={{0,8},{1,9},{2,10},{3,11},{4,12},{5,13},{6,14},{7,15},{8,0},{9,1},... | collective-permute-start | bytes 589832 | tf_op jit(solution)/shard_map/ppermute | solution.py:82
  40.9 4.9 %collective-permute-done.13 = bf16[128,768]{1,0:T(8,128)(2,1)S(1)} collective-permute-done((bf16[128,768]{1,0:T(8,128)(2,1)S(1)}, bf16[128,768]{1,0:T(8,128)(2,1)S(1)}, u32[]{:S(2)}, u32[]{:S(2)}) %collective-permute-start.13) | collective-permute-done | bytes 196640 | tf_op jit(solution)/shard_map/ppermute | solution.py:82
  46.8 1.8 %collective-permute-start.14 = (bf16[128,768]{1,0:T(8,128)(2,1)S(1)}, bf16[128,768]{1,0:T(8,128)(2,1)S(1)}, u32[]{:S(2)}, u32[]{:S(2)}) collective-permute-start(bf16[128,768]{1,0:T(8,128)(2,1)S(1)} %maximum_convert_fusion.refs_7_), channel_id=1, source_target_pairs={{0,8},{1,9},{2,10},{3,11},{4,12},{5,13},{6,14},{7,15},{8,0},{9,1},... | collective-permute-start | bytes 589832 | tf_op jit(solution)/shard_map/ppermute | solution.py:82
  50.1 1.7 %collective-permute-start.15 = (bf16[128,768]{1,0:T(8,128)(2,1)S(1)}, bf16[128,768]{1,0:T(8,128)(2,1)S(1)}, u32[]{:S(2)}, u32[]{:S(2)}) collective-permute-start(bf16[128,768]{1,0:T(8,128)(2,1)S(1)} %maximum_convert_fusion.refs_7_), channel_id=1, source_target_pairs={{0,16},{1,17},{2,18},{3,19},{4,20},{5,21},{6,22},{7,23},{8,24},{9,... | collective-permute-start | bytes 589832 | tf_op jit(solution)/shard_map/ppermute | solution.py:82
  54.4 3.1 %collective-permute-done.9.refs_5_ = bf16[128,768]{1,0:T(8,128)(2,1)S(1)} collective-permute-done((bf16[128,768]{1,0:T(8,128)(2,1)S(1)}, bf16[128,768]{1,0:T(8,128)(2,1)S(1)}, u32[]{:S(2)}, u32[]{:S(2)}) %collective-permute-start.9) | collective-permute-done | bytes 196640 | tf_op jit(solution)/shard_map/ppermute | solution.py:82
  57.8 3.5 %collective-permute-done.15.refs_9_ = bf16[128,768]{1,0:T(8,128)(2,1)S(1)} collective-permute-done((bf16[128,768]{1,0:T(8,128)(2,1)S(1)}, bf16[128,768]{1,0:T(8,128)(2,1)S(1)}, u32[]{:S(2)}, u32[]{:S(2)}) %collective-permute-start.15) | collective-permute-done | bytes 196640 | tf_op jit(solution)/shard_map/ppermute | solution.py:82
  61.3 2.1 %collective-permute-done.16.refs_10_ = bf16[128,768]{1,0:T(8,128)(2,1)S(1)} collective-permute-done((bf16[128,768]{1,0:T(8,128)(2,1)S(1)}, bf16[128,768]{1,0:T(8,128)(2,1)S(1)}, u32[]{:S(2)}, u32[]{:S(2)}) %collective-permute-start.16) | collective-permute-done | bytes 196640 | tf_op jit(solution)/shard_map/ppermute | solution.py:82
  64.8 5.2 %down.1 = (bf16[4,128,192]{2,1,0:T(8,128)(2,1)}, bf16[4,128,192]{2,1,0:T(8,128)(2,1)}) custom-call(s32[2]{0:T(128)} %pad_add_fusion.refs_0_, bf16[4,128,200]{2,1,0:T(8,128)(2,1)} %copy-done.1, bf16[4,384,768]{2,1,0:T(8,128)(2,1)} %refs_2_.1, bf16[128,768]{1,0:T(8,128)(2,1)} %copy-done.3, bf16[128,768]{1,0:T(8,128)(2,1)} %copy-done.8, ...), custom_call_target="tpu_custom_call" | custom-call | tf_op jit(solution)/shard_map/down/pallas_call | solution.py:219
  70.1 1.7 %collective-permute-done.17 = bf16[4,128,192]{2,1,0:T(8,128)(2,1)S(1)} collective-permute-done((bf16[4,128,192]{2,1,0:T(8,128)(2,1)}, bf16[4,128,192]{2,1,0:T(8,128)(2,1)S(1)}, u32[]{:S(2)}, u32[]{:S(2)}) %collective-permute-start.17) | collective-permute-done | bytes 196640 | tf_op jit(solution)/shard_map/ppermute | solution.py:82
  73.5 2.6 %collective-permute-start.19 = (bf16[128,192]{1,0:T(8,128)(2,1)S(1)}, bf16[128,192]{1,0:T(8,128)(2,1)S(1)}, u32[]{:S(2)}, u32[]{:S(2)}) collective-permute-start(bf16[128,192]{1,0:T(8,128)(2,1)S(1)} %get-tuple-element.31), channel_id=1, source_target_pairs={{0,8},{1,9},{2,0},{3,1},{4,24},{5,25},{6,16},{7,17},{8,10},{9,11},... | collective-permute-start | bytes 147464 | tf_op jit(solution)/shard_map/ppermute | solution.py:82
  76.1 3.0 %collective-permute-start.20 = (bf16[128,192]{1,0:T(8,128)(2,1)S(1)}, bf16[128,192]{1,0:T(8,128)(2,1)S(1)}, u32[]{:S(2)}, u32[]{:S(2)}) collective-permute-start(bf16[128,192]{1,0:T(8,128)(2,1)S(1)} %get-tuple-element.30), channel_id=1, source_target_pairs={{0,16},{1,17},{2,24},{3,25},{4,0},{5,1},{6,8},{7,9},{8,18},{9,19},... | collective-permute-start | bytes 147464 | tf_op jit(solution)/shard_map/ppermute | solution.py:82
  80.0 12.4 %collective-permute-done.19 = bf16[128,192]{1,0:T(8,128)(2,1)S(1)} collective-permute-done((bf16[128,192]{1,0:T(8,128)(2,1)S(1)}, bf16[128,192]{1,0:T(8,128)(2,1)S(1)}, u32[]{:S(2)}, u32[]{:S(2)}) %collective-permute-start.19) | collective-permute-done | bytes 49184 | tf_op jit(solution)/shard_map/ppermute | solution.py:82
  94.1 1.6 %collective-permute-start.23 = (bf16[16,768]{1,0:T(8,128)(2,1)S(1)}, bf16[16,768]{1,0:T(8,128)(2,1)S(1)}, u32[]{:S(2)}, u32[]{:S(2)}) collective-permute-start(bf16[16,768]{1,0:T(8,128)(2,1)S(1)} %get-tuple-element.32), channel_id=1, source_target_pairs={{0,2},{1,3},{2,0},{3,1},{4,6},{5,7},{6,4},{7,5},{8,10},{9,11},{10,... | collective-permute-start | bytes 73736 | tf_op jit(solution)/shard_map/ppermute | solution.py:82
  95.7 3.1 %collective-permute-start.24 = (bf16[16,768]{1,0:T(8,128)(2,1)S(1)}, bf16[16,768]{1,0:T(8,128)(2,1)S(1)}, u32[]{:S(2)}, u32[]{:S(2)}) collective-permute-start(bf16[16,768]{1,0:T(8,128)(2,1)S(1)} %get-tuple-element.34), channel_id=1, source_target_pairs={{0,4},{1,5},{2,6},{3,7},{4,0},{5,1},{6,2},{7,3},{8,12},{9,13},{10,... | collective-permute-start | bytes 73736 | tf_op jit(solution)/shard_map/ppermute | solution.py:82
  100.6 3.8 %collective-permute-done.25 = bf16[16,768]{1,0:T(8,128)(2,1)S(1)} collective-permute-done((bf16[16,768]{1,0:T(8,128)(2,1)S(1)}, bf16[16,768]{1,0:T(8,128)(2,1)S(1)}, u32[]{:S(2)}, u32[]{:S(2)}) %collective-permute-start.25) | collective-permute-done | bytes 24608 | tf_op jit(solution)/shard_map/ppermute | solution.py:82
  (90 shorter events, 22.5 us)
Async XLA Ops:
  4.1 11.8 %collective-permute-start = (bf16[128,200]{1,0:T(8,128)(2,1)S(1)}, bf16[128,200]{1,0:T(8,128)(2,1)S(1)}, u32[]{:S(2)}, u32[]{:S(2)}) collective-permute-start(bf16[128,200]{1,0:T(8,128)(2,1)S(1)} %concatenate.3), channel_id=1, source_target_pairs={{0,0},{1,1},{2,8},{3,9},{4,16},{5,17},{6,24},{7,25},{8,2},{9,3},{1... | collective-permute-start | bytes 153608 | tf_op jit(solution)/shard_map/ppermute | solution.py:82
  4.8 11.1 %collective-permute-start.1 = (bf16[128,200]{1,0:T(8,128)(2,1)S(1)}, bf16[128,200]{1,0:T(8,128)(2,1)S(1)}, u32[]{:S(2)}, u32[]{:S(2)}) collective-permute-start(bf16[128,200]{1,0:T(8,128)(2,1)S(1)} %concatenate.3), channel_id=1, source_target_pairs={{0,2},{1,3},{2,10},{3,11},{4,18},{5,19},{6,26},{7,27},{8,0},{9,1},... | collective-permute-start | bytes 153608 | tf_op jit(solution)/shard_map/ppermute | solution.py:82
  10.5 7.2 %collective-permute-start.2 = (bf16[128,200]{1,0:T(8,128)(2,1)S(1)}, bf16[128,200]{1,0:T(8,128)(2,1)S(1)}, u32[]{:S(2)}, u32[]{:S(2)}) collective-permute-start(bf16[128,200]{1,0:T(8,128)(2,1)S(1)} %concatenate.3), channel_id=1, source_target_pairs={{0,4},{1,5},{2,12},{3,13},{4,20},{5,21},{6,28},{7,29},{8,6},{9,7},... | collective-permute-start | bytes 153608 | tf_op jit(solution)/shard_map/ppermute | solution.py:82
  14.0 5.2 %collective-permute-start.3 = (bf16[128,200]{1,0:T(8,128)(2,1)S(1)}, bf16[128,200]{1,0:T(8,128)(2,1)S(1)}, u32[]{:S(2)}, u32[]{:S(2)}) collective-permute-start(bf16[128,200]{1,0:T(8,128)(2,1)S(1)} %concatenate.3), channel_id=1, source_target_pairs={{0,6},{1,7},{2,14},{3,15},{4,22},{5,23},{6,30},{7,31},{8,4},{9,5},... | collective-permute-start | bytes 153608 | tf_op jit(solution)/shard_map/ppermute | solution.py:82
  26.4 9.3 %collective-permute-start.12 = (bf16[128,768]{1,0:T(8,128)(2,1)}, bf16[128,768]{1,0:T(8,128)(2,1)S(1)}, u32[]{:S(2)}, u32[]{:S(2)}) collective-permute-start(bf16[128,768]{1,0:T(8,128)(2,1)} %get-tuple-element.19), channel_id=1, source_target_pairs={{0,16},{1,17},{2,18},{3,19},{4,20},{5,21},{6,22},{7,23},{8,24},{9,... | collective-permute-start | bytes 589832 | tf_op jit(solution)/shard_map/ppermute | solution.py:82
  29.8 11.1 %collective-permute-start.11 = (bf16[128,768]{1,0:T(8,128)(2,1)}, bf16[128,768]{1,0:T(8,128)(2,1)S(1)}, u32[]{:S(2)}, u32[]{:S(2)}) collective-permute-start(bf16[128,768]{1,0:T(8,128)(2,1)} %get-tuple-element.17), channel_id=1, source_target_pairs={{0,16},{1,17},{2,18},{3,19},{4,20},{5,21},{6,22},{7,23},{8,24},{9,... | collective-permute-start | bytes 589832 | tf_op jit(solution)/shard_map/ppermute | solution.py:82
  29.8 9.7 %collective-permute-start.6 = (bf16[128,768]{1,0:T(8,128)(2,1)}, bf16[128,768]{1,0:T(8,128)(2,1)S(1)}, u32[]{:S(2)}, u32[]{:S(2)}) collective-permute-start(bf16[128,768]{1,0:T(8,128)(2,1)} %get-tuple-element.15), channel_id=1, source_target_pairs={{0,8},{1,9},{2,10},{3,11},{4,12},{5,13},{6,14},{7,15},{8,0},{9,1},... | collective-permute-start | bytes 589832 | tf_op jit(solution)/shard_map/ppermute | solution.py:82
  32.5 16.1 %collective-permute-start.5 = (bf16[128,768]{1,0:T(8,128)(2,1)}, bf16[128,768]{1,0:T(8,128)(2,1)S(1)}, u32[]{:S(2)}, u32[]{:S(2)}) collective-permute-start(bf16[128,768]{1,0:T(8,128)(2,1)} %get-tuple-element.13), channel_id=1, source_target_pairs={{0,8},{1,9},{2,10},{3,11},{4,12},{5,13},{6,14},{7,15},{8,0},{9,1},... | collective-permute-start | bytes 589832 | tf_op jit(solution)/shard_map/ppermute | solution.py:82
  36.7 9.1 %collective-permute-start.13 = (bf16[128,768]{1,0:T(8,128)(2,1)S(1)}, bf16[128,768]{1,0:T(8,128)(2,1)S(1)}, u32[]{:S(2)}, u32[]{:S(2)}) collective-permute-start(bf16[128,768]{1,0:T(8,128)(2,1)S(1)} %add_convert_fusion.1), channel_id=1, source_target_pairs={{0,8},{1,9},{2,10},{3,11},{4,12},{5,13},{6,14},{7,15},{8,0},{9,1},... | collective-permute-start | bytes 589832 | tf_op jit(solution)/shard_map/ppermute | solution.py:82
  40.5 8.1 %collective-permute-start.7 = (bf16[128,768]{1,0:T(8,128)(2,1)S(1)}, bf16[128,768]{1,0:T(8,128)(2,1)S(1)}, u32[]{:S(2)}, u32[]{:S(2)}) collective-permute-start(bf16[128,768]{1,0:T(8,128)(2,1)S(1)} %add_convert_fusion.2), channel_id=1, source_target_pairs={{0,16},{1,17},{2,18},{3,19},{4,20},{5,21},{6,22},{7,23},{8,24},{9,... | collective-permute-start | bytes 589832 | tf_op jit(solution)/shard_map/ppermute | solution.py:82
  46.8 6.5 %collective-permute-start.14 = (bf16[128,768]{1,0:T(8,128)(2,1)S(1)}, bf16[128,768]{1,0:T(8,128)(2,1)S(1)}, u32[]{:S(2)}, u32[]{:S(2)}) collective-permute-start(bf16[128,768]{1,0:T(8,128)(2,1)S(1)} %maximum_convert_fusion.refs_7_), channel_id=1, source_target_pairs={{0,8},{1,9},{2,10},{3,11},{4,12},{5,13},{6,14},{7,15},{8,0},{9,1},... | collective-permute-start | bytes 589832 | tf_op jit(solution)/shard_map/ppermute | solution.py:82
  49.7 7.8 %collective-permute-start.9 = (bf16[128,768]{1,0:T(8,128)(2,1)S(1)}, bf16[128,768]{1,0:T(8,128)(2,1)S(1)}, u32[]{:S(2)}, u32[]{:S(2)}) collective-permute-start(bf16[128,768]{1,0:T(8,128)(2,1)S(1)} %maximum_convert_fusion.1.refs_3_), channel_id=1, source_target_pairs={{0,16},{1,17},{2,18},{3,19},{4,20},{5,21},{6,22},{7,23},{8,24},{9,... | collective-permute-start | bytes 589832 | tf_op jit(solution)/shard_map/ppermute | solution.py:82
  50.1 11.3 %collective-permute-start.15 = (bf16[128,768]{1,0:T(8,128)(2,1)S(1)}, bf16[128,768]{1,0:T(8,128)(2,1)S(1)}, u32[]{:S(2)}, u32[]{:S(2)}) collective-permute-start(bf16[128,768]{1,0:T(8,128)(2,1)S(1)} %maximum_convert_fusion.refs_7_), channel_id=1, source_target_pairs={{0,16},{1,17},{2,18},{3,19},{4,20},{5,21},{6,22},{7,23},{8,24},{9,... | collective-permute-start | bytes 589832 | tf_op jit(solution)/shard_map/ppermute | solution.py:82
  51.8 9.5 %collective-permute-start.8 = (bf16[128,768]{1,0:T(8,128)(2,1)S(1)}, bf16[128,768]{1,0:T(8,128)(2,1)S(1)}, u32[]{:S(2)}, u32[]{:S(2)}) collective-permute-start(bf16[128,768]{1,0:T(8,128)(2,1)S(1)} %maximum_convert_fusion.1.refs_3_), channel_id=1, source_target_pairs={{0,8},{1,9},{2,10},{3,11},{4,12},{5,13},{6,14},{7,15},{8,0},{9,1},... | collective-permute-start | bytes 589832 | tf_op jit(solution)/shard_map/ppermute | solution.py:82
  53.3 10.1 %collective-permute-start.16 = (bf16[128,768]{1,0:T(8,128)(2,1)S(1)}, bf16[128,768]{1,0:T(8,128)(2,1)S(1)}, u32[]{:S(2)}, u32[]{:S(2)}) collective-permute-start(bf16[128,768]{1,0:T(8,128)(2,1)S(1)} %collective-permute-done.14.refs_8_), channel_id=1, source_target_pairs={{0,16},{1,17},{2,18},{3,19},{4,20},{5,21},{6,22},{7,23},{8,24},{9,... | collective-permute-start | bytes 589832 | tf_op jit(solution)/shard_map/ppermute | solution.py:82
  57.5 5.9 %collective-permute-start.10 = (bf16[128,768]{1,0:T(8,128)(2,1)S(1)}, bf16[128,768]{1,0:T(8,128)(2,1)S(1)}, u32[]{:S(2)}, u32[]{:S(2)}) collective-permute-start(bf16[128,768]{1,0:T(8,128)(2,1)S(1)} %collective-permute-done.9.refs_5_), channel_id=1, source_target_pairs={{0,8},{1,9},{2,10},{3,11},{4,12},{5,13},{6,14},{7,15},{8,0},{9,1},... | collective-permute-start | bytes 589832 | tf_op jit(solution)/shard_map/ppermute | solution.py:82
  70.0 1.8 %collective-permute-start.17 = (bf16[4,128,192]{2,1,0:T(8,128)(2,1)}, bf16[4,128,192]{2,1,0:T(8,128)(2,1)S(1)}, u32[]{:S(2)}, u32[]{:S(2)}) collective-permute-start(bf16[4,128,192]{2,1,0:T(8,128)(2,1)} %get-tuple-element.21), channel_id=1, source_target_pairs={{0,1},{1,0},{2,3},{3,2},{4,5},{5,4},{6,7},{7,6},{8,9},{9,8},{10,11... | collective-permute-start | bytes 589832 | tf_op jit(solution)/shard_map/ppermute | solution.py:82
  72.9 7.1 %collective-permute-start.18 = (bf16[128,192]{1,0:T(8,128)(2,1)S(1)}, bf16[128,192]{1,0:T(8,128)(2,1)S(1)}, u32[]{:S(2)}, u32[]{:S(2)}) collective-permute-start(bf16[128,192]{1,0:T(8,128)(2,1)S(1)} %get-tuple-element.28), channel_id=1, source_target_pairs={{0,0},{1,1},{2,8},{3,9},{4,16},{5,17},{6,24},{7,25},{8,2},{9,3},{1... | collective-permute-start | bytes 147464 | tf_op jit(solution)/shard_map/ppermute | solution.py:82
  73.5 18.8 %collective-permute-start.19 = (bf16[128,192]{1,0:T(8,128)(2,1)S(1)}, bf16[128,192]{1,0:T(8,128)(2,1)S(1)}, u32[]{:S(2)}, u32[]{:S(2)}) collective-permute-start(bf16[128,192]{1,0:T(8,128)(2,1)S(1)} %get-tuple-element.31), channel_id=1, source_target_pairs={{0,8},{1,9},{2,0},{3,1},{4,24},{5,25},{6,16},{7,17},{8,10},{9,11},... | collective-permute-start | bytes 147464 | tf_op jit(solution)/shard_map/ppermute | solution.py:82
  76.1 16.2 %collective-permute-start.20 = (bf16[128,192]{1,0:T(8,128)(2,1)S(1)}, bf16[128,192]{1,0:T(8,128)(2,1)S(1)}, u32[]{:S(2)}, u32[]{:S(2)}) collective-permute-start(bf16[128,192]{1,0:T(8,128)(2,1)S(1)} %get-tuple-element.30), channel_id=1, source_target_pairs={{0,16},{1,17},{2,24},{3,25},{4,0},{5,1},{6,8},{7,9},{8,18},{9,19},... | collective-permute-start | bytes 147464 | tf_op jit(solution)/shard_map/ppermute | solution.py:82
  79.1 13.3 %collective-permute-start.21 = (bf16[128,192]{1,0:T(8,128)(2,1)S(1)}, bf16[128,192]{1,0:T(8,128)(2,1)S(1)}, u32[]{:S(2)}, u32[]{:S(2)}) collective-permute-start(bf16[128,192]{1,0:T(8,128)(2,1)S(1)} %get-tuple-element.29), channel_id=1, source_target_pairs={{0,24},{1,25},{2,16},{3,17},{4,8},{5,9},{6,0},{7,1},{8,26},{9,27},... | collective-permute-start | bytes 147464 | tf_op jit(solution)/shard_map/ppermute | solution.py:82
  94.1 5.4 %collective-permute-start.23 = (bf16[16,768]{1,0:T(8,128)(2,1)S(1)}, bf16[16,768]{1,0:T(8,128)(2,1)S(1)}, u32[]{:S(2)}, u32[]{:S(2)}) collective-permute-start(bf16[16,768]{1,0:T(8,128)(2,1)S(1)} %get-tuple-element.32), channel_id=1, source_target_pairs={{0,2},{1,3},{2,0},{3,1},{4,6},{5,7},{6,4},{7,5},{8,10},{9,11},{10,... | collective-permute-start | bytes 73736 | tf_op jit(solution)/shard_map/ppermute | solution.py:82
  95.7 4.9 %collective-permute-start.24 = (bf16[16,768]{1,0:T(8,128)(2,1)S(1)}, bf16[16,768]{1,0:T(8,128)(2,1)S(1)}, u32[]{:S(2)}, u32[]{:S(2)}) collective-permute-start(bf16[16,768]{1,0:T(8,128)(2,1)S(1)} %get-tuple-element.34), channel_id=1, source_target_pairs={{0,4},{1,5},{2,6},{3,7},{4,0},{5,1},{6,2},{7,3},{8,12},{9,13},{10,... | collective-permute-start | bytes 73736 | tf_op jit(solution)/shard_map/ppermute | solution.py:82
  98.8 5.6 %collective-permute-start.25 = (bf16[16,768]{1,0:T(8,128)(2,1)S(1)}, bf16[16,768]{1,0:T(8,128)(2,1)S(1)}, u32[]{:S(2)}, u32[]{:S(2)}) collective-permute-start(bf16[16,768]{1,0:T(8,128)(2,1)S(1)} %get-tuple-element.33), channel_id=1, source_target_pairs={{0,6},{1,7},{2,4},{3,5},{4,2},{5,3},{6,0},{7,1},{8,14},{9,15},{10,... | collective-permute-start | bytes 73736 | tf_op jit(solution)/shard_map/ppermute | solution.py:82
  (16 other events, 252.6 us)

commit v2 on v0

--- a/solution.py
+++ b/solution.py
@@ -1,7 +1,16 @@
+import functools
+
 import jax
 import jax.numpy as jnp
 from jax import lax
+from jax.experimental import pallas as pl
+from jax.experimental.pallas import tpu as pltpu
 from jax.sharding import PartitionSpec as P
+
+
+ALL = ("expert", "tensor", "rep")
+F32 = jnp.float32
+BF16 = jnp.bfloat16
 
 
 def tower_head(pre, tower_bias, tower_out, out_bias):
@@ -11,7 +20,7 @@
     return jax.nn.sigmoid(logits).T
 
 
-def per_device(
+def moved_weights(
     requests, expert_ids, gate_values, w_up, w_down, tower_in, tower_bias, tower_out, out_bias
 ):
     groups = lax.axis_size("expert")
@@ -63,7 +72,379 @@
     return (mixed, scores)
 
 
+def permute(x, move):
+    sizes = [lax.axis_size(a) for a in ALL]
+    pairs = []
+    for e in range(sizes[0]):
+        for t in range(sizes[1]):
+            for r in range(sizes[2]):
+                e2, t2, r2 = move(e, t, r)
+                pairs.append(
+                    ((e * sizes[1] + t) * sizes[2] + r, (e2 * sizes[1] + t2) * sizes[2] + r2)
+                )
+    return lax.ppermute(x, ALL, pairs)
+
+
+NT = (((1,), (1,)), ((), ()))
+LANES = 128
+VMEM = pl.BlockSpec(memory_space=pltpu.VMEM)
+PLAIN = pl.BlockSpec(memory_space=pltpu.VMEM)
+SMEM = pl.BlockSpec(memory_space=pltpu.SMEM)
+ANY = pl.BlockSpec(memory_space=pl.ANY)
+SMALL = pltpu.CompilerParams(vmem_limit_bytes=20 << 20)
+META = 16
+
+
+def call(kernel, outs, operands, scratch=(), **static):
+    specs, arrays = [], []
+    for item in operands:
+        spec, array = item if isinstance(item, tuple) else (VMEM, item)
+        if spec is VMEM:
+            array = pltpu.with_memory_space_constraint(array, pltpu.VMEM)
+        specs.append(spec)
+        arrays.append(array)
+    return pl.pallas_call(
+        functools.partial(kernel, **static),
+        out_shape=[pltpu.VMEM(*o) for o in outs],
+        in_specs=specs,
+        out_specs=[VMEM] * len(outs),
+        scratch_shapes=list(scratch),
+        compiler_params=SMALL,
+    )(*arrays)
+
+
+def pack_kernel(req_ref, ids_ref, gates_ref, out_ref):
+    width, tok = req_ref.shape
+    out_ref[:width, :] = req_ref[...]
+    gates = gates_ref[...]
+    high = gates.astype(BF16).astype(F32)
+    left = gates - high
+    mid = left.astype(BF16).astype(F32)
+    low = left - mid
+    ids = ids_ref[...].astype(F32)
+    fill = jnp.zeros((META - 8, tok), F32)
+    out_ref[width:, :] = jnp.concatenate([ids, high, mid, low, fill], axis=0).astype(BF16)
+
+
+def here():
+    e, t, r = (lax.axis_index(name) for name in ALL)
+    return jnp.bitwise_xor(e, t), t, r
+
+
+def load_kernel(w_ref, out_ref, sem):
+    copy = pltpu.make_async_copy(w_ref, out_ref, sem)
+    copy.start()
+    copy.wait()
+
+
+def prepare_kernel(w_ref, mine_ref, other_ref, out_ref, tower_ref, sem):
+    width = mine_ref.shape[0]
+    _, _, r = here()
+    copy = pltpu.make_async_copy(w_ref, out_ref, sem)
+    copy.start()
+    tower_ref[pl.ds(pl.multiple_of(r * width, width), width), :] = mine_ref[...]
+    tower_ref[pl.ds(pl.multiple_of((1 - r) * width, width), width), :] = other_ref[...]
+    copy.wait()
+
+
+def fetch(own, other, so, sp, blocks, width):
+    for k in range(blocks):
+        so[k] = own[k][...]
+        sp[k] = other[k][:width, :]
+
+
+def arrange(so, sp, src, r, width, part):
+    a, b = so[src, :width, :], sp[src]
+    low = jnp.where(r == 0, a, b)
+    high = jnp.where(r == 0, b, a)
+    x = jnp.concatenate([low, high], axis=0).T
+    cols = so[src, width:, :].astype(F32).T.astype(BF16)
+
+    def order(v):
+        groups = v.shape[0] // part
+        pieces = [v[g * part : (g + 1) * part, :] for h in (0, 1) for g in range(h, groups, 2)]
+        return jnp.concatenate(pieces, axis=0)
+
+    return order(x), order(cols)
+
+
+def project(x, cols, w_ref, acc, outs, tok):
+    experts, _, hid = w_ref.shape
+    tile = 2 * LANES
+    for n in range(0, hid, tile):
+        for j in range(experts):
+            part = jnp.dot(x, w_ref[j, :, n : n + tile], preferred_element_type=F32).astype(BF16)
+            for k in range(2):
+                new = part
+                if j:
+                    hit = cols[:, k : k + 1] == jnp.asarray(j, BF16)
+                    new = jnp.where(hit, part, acc[k])
+                if j < experts - 1:
+                    acc[k] = new
+                else:
+                    for m, out in enumerate(outs[k]):
+                        out[:, n : n + tile] = new[m * tok : (m + 1) * tok, :]
+
+
+def far_kernel(*refs, blocks, part):
+    own, other, w_ref = refs[:blocks], refs[blocks : 2 * blocks], refs[2 * blocks]
+    a_ref, b_ref, so, sp, acc = refs[2 * blocks + 1 :]
+    width, tok = w_ref.shape[1] // 2, own[0].shape[1]
+    flip, _, r = here()
+    fetch(own, other, so, sp, blocks, width)
+    x, cols = arrange(so, sp, jnp.bitwise_xor(flip, blocks - 1), r, width, part)
+    project(x, cols, w_ref, acc, ([a_ref], [b_ref]), tok)
+
+
+def near_kernel(*refs, blocks, part):
+    own, other, w_ref = refs[:blocks], refs[blocks : 2 * blocks], refs[2 * blocks]
+    near = blocks - 1
+    outs, rest = refs[2 * blocks + 1 : 2 * blocks + 1 + 2 * near], refs[2 * blocks + 1 + 2 * near :]
+    meta_ref, so, sp, acc, x = rest
+    width, tok = w_ref.shape[1] // 2, own[0].shape[1]
+    flip, _, r = here()
+    fetch(own, other, so, sp, blocks, width)
+    for m in range(blocks):
+        rows, cols = arrange(so, sp, jnp.bitwise_xor(flip, m), r, width, part)
+        if m < near:
+            x[m * tok : (m + 1) * tok, :] = rows
+        meta_ref[m * tok : (m + 1) * tok, :] = cols
+    project(x[...], meta_ref[: near * tok, :], w_ref, acc, (outs[:near], outs[near:]), tok)
+
+
+def down_kernel(*refs, blocks, mine):
+    meta_ref, hidden, w_ref = refs[0], refs[1 : 1 + 2 * blocks], refs[1 + 2 * blocks]
+    out_ref, h0, h1, mt = refs[2 + 2 * blocks :]
+    experts = w_ref.shape[0]
+    tok = hidden[0].shape[0]
+    half = tok // 2
+    _, _, r = here()
+    side = r if mine else 1 - r
+    for m in range(blocks):
+        rows, at = slice(m * half, (m + 1) * half), pl.multiple_of(side * half, half)
+        h0[rows, :] = hidden[m][pl.ds(at, half), :]
+        h1[rows, :] = hidden[blocks + m][pl.ds(at, half), :]
+        mt[rows, :] = meta_ref[pl.ds(pl.multiple_of(m * tok + at, half), half), :]
+    meta = mt[...]
+    gates = []
+    for k in range(2):
+        three = [meta[:, 2 * q + k : 2 * q + k + 1].astype(F32) for q in (1, 2, 3)]
+        gates.append(three[0] + three[1] + three[2])
+    ids = [meta[:, k : k + 1].astype(F32) for k in range(2)]
+    zero = jnp.zeros(h0.shape, BF16)
+    total = None
+    for j in range(experts):
+        first, second = (meta[:, k : k + 1] == jnp.asarray(j, BF16) for k in range(2))
+        rows = jnp.where(first, h0[...], jnp.where(second, h1[...], zero))
+        gate = jnp.where(ids[0] == float(j), gates[0], jnp.where(ids[1] == float(j), gates[1], 0.0))
+        part = gate * lax.dot_general(rows, w_ref[j], NT, preferred_element_type=F32)
+        total = part if total is None else total + part
+    for m in range(blocks):
+        out_ref[m] = total[m * half : (m + 1) * half, :].astype(BF16)
+
+
+def add_kernel(a_ref, b_ref, *outs):
+    for m, out in enumerate(outs):
+        out[...] = (a_ref[m].astype(F32) + b_ref[m].astype(F32)).astype(BF16)
+
+
+def route_kernel(*refs, blocks):
+    pieces, outs, sp = refs[:blocks], refs[blocks : 2 * blocks], refs[2 * blocks]
+    flip, _, _ = here()
+    for m in range(blocks):
+        sp[m] = pieces[m][...]
+    for k in range(blocks):
+        outs[k][...] = sp[jnp.bitwise_xor(flip, k)]
+
+
+def tower_kernel(*refs, blocks):
+    got, tower_ref = refs[:blocks], refs[blocks]
+    mine_ref, theirs_ref = refs[blocks + 1 : blocks + 3]
+    outs, pre = refs[blocks + 3 : 2 * blocks + 3], refs[2 * blocks + 3]
+    _, t, r = here()
+    width = mine_ref.shape[1]
+    part = outs[0].shape[0]
+    total = got[0][...].astype(F32)
+    for g in got[1:]:
+        total = total + g[...].astype(F32)
+    mixed = total.astype(BF16)
+    pre[...] = jnp.dot(mixed, tower_ref[...], preferred_element_type=F32)
+    for k in range(blocks):
+        at = pl.multiple_of(jnp.bitwise_xor(t, k) * part, part)
+        outs[k][...] = pre[pl.ds(at, part), :].astype(BF16)
+    low, high = mixed[:, :width], mixed[:, width:]
+    mine_ref[...] = jnp.where(r == 0, low, high)
+    theirs_ref[...] = jnp.where(r == 0, high, low)
+
+
+def mixed_kernel(mine_ref, recv_ref, out_ref, both, *, part):
+    _, _, r = here()
+    for g in range(mine_ref.shape[0] // part):
+        rows = slice(g * part, (g + 1) * part)
+        both[pl.ds(pl.multiple_of((2 * g + r) * part, part), part), :] = mine_ref[rows, :]
+        both[pl.ds(pl.multiple_of((2 * g + 1 - r) * part, part), part), :] = recv_ref[rows, :]
+    out_ref[...] = both[...].T
+
+
+def head_kernel(*refs, blocks):
+    got, (bias_ref, tower_ref, last_ref, score_ref) = refs[:blocks], refs[blocks:]
+    tasks, units = tower_ref.shape
+    total = got[0][...].astype(F32)
+    for g in got[1:]:
+        total = total + g[...].astype(F32)
+    rows = []
+    for j in range(tasks):
+        act = None
+        for c in range(units // LANES):
+            at = j * units + c * LANES
+            pre = total[:, at : at + LANES] + bias_ref[at : at + LANES].reshape(1, LANES)
+            one = jnp.maximum(pre, 0.0) * tower_ref[j : j + 1, c * LANES : (c + 1) * LANES]
+            act = one if act is None else act + one
+        rows.append(jnp.sum(act.T, axis=0, keepdims=True) + last_ref[0, j])
+    score_ref[...] = jax.nn.sigmoid(jnp.concatenate(rows, axis=0))
+
+
+def stationary(
+    requests, expert_ids, gate_values, w_up, w_down, tower_in, tower_bias, tower_out, out_bias
+):
+    blocks, reps = lax.axis_size("expert"), lax.axis_size("rep")
+    tok, width = requests.shape
+    _, span, hid = w_up.shape
+    units = tower_in.shape[1]
+    part = tok // (blocks * reps)
+    half = tok // reps
+
+    def x_of(v):
+        return permute(v, lambda e, t, r: (e ^ 1, t, r))
+
+    def y_of(v):
+        return permute(v, lambda e, t, r: (e ^ 2, t, r))
+
+    def xy_of(v):
+        return permute(v, lambda e, t, r: (e ^ 3, t, r))
+
+    def z_of(v, k):
+        return permute(v, lambda e, t, r: (e, t ^ k, r))
+
+    def r_of(v):
+        return permute(v, lambda e, t, r: (e, t, 1 - r))
+
+    (packed,) = call(
+        pack_kernel,
+        [((width + META, tok), BF16)],
+        [(PLAIN, v.T) for v in (requests, expert_ids, gate_values)],
+    )
+    own = [permute(packed, lambda e, t, r, k=k: (t, e ^ k, r)) for k in range(blocks)]
+    one = [pltpu.SemaphoreType.DMA(())]
+    (up,) = call(load_kernel, [(w_up.shape, BF16)], [(ANY, w_up)], one)
+    other = [r_of(v) for v in own]
+
+    slab = ((tok, hid), BF16)
+    stage = [
+        pltpu.VMEM((blocks, width + META, tok), BF16),
+        pltpu.VMEM((blocks, width, tok), BF16),
+    ]
+    near = blocks - 1
+    ad, bd = call(
+        far_kernel,
+        [slab] * 2,
+        own + other + [up],
+        stage + [pltpu.VMEM((2, tok, 2 * LANES), BF16)],
+        blocks=blocks,
+        part=part,
+    )
+    rad, rbd = x_of(ad), y_of(bd)
+    *parts, meta = call(
+        near_kernel,
+        [slab] * (2 * near) + [((blocks * tok, META), BF16)],
+        own + other + [up],
+        stage
+        + [
+            pltpu.VMEM((2, near * tok, 2 * LANES), BF16),
+            pltpu.VMEM((near * tok, span), BF16),
+        ],
+        blocks=blocks,
+        part=part,
+    )
+    (ao, an, ay), (bo, bx, bn) = parts[:near], parts[near:]
+
+    ran, rbn = x_of(an), y_of(bn)
+    fa = (ay.astype(F32) + rad.astype(F32)).astype(BF16)
+    fb = (bx.astype(F32) + rbd.astype(F32)).astype(BF16)
+    ra2, rb2 = y_of(fa), x_of(fb)
+    ha = jax.nn.relu(ao.astype(F32) + ran.astype(F32) + ra2.astype(F32)).astype(BF16)
+    hb = jax.nn.relu(bo.astype(F32) + rbn.astype(F32) + rb2.astype(F32)).astype(BF16)
+
+    hax, hay = x_of(ha), y_of(ha)
+    hbx, hby = x_of(hb), y_of(hb)
+    haxy, hbxy = x_of(hay), y_of(hbx)
+    tower_other = r_of(tower_in)
+    down, tower = call(
+        prepare_kernel,
+        [(w_down.shape, BF16), ((span, units), BF16)],
+        [(ANY, w_down), (PLAIN, tower_in), tower_other],
+        one,
+    )
+
+    cut = ((blocks, half, span), BF16)
+    operands = [meta, ha, hax, hay, haxy, hb, hbx, hby, hbxy, down]
+    scratch = [pltpu.VMEM((blocks * half, hid), BF16)] * 2
+    scratch.append(pltpu.VMEM((blocks * half, META), BF16))
+    (send,) = call(down_kernel, [cut], operands, scratch, blocks=blocks, mine=False)
+    recv = r_of(send)
+    (keep,) = call(down_kernel, [cut], operands, scratch, blocks=blocks, mine=True)
+    slab = ((half, span), BF16)
+    b0, b1, b2, b3 = call(add_kernel, [slab] * blocks, [keep, recv])
+    p3 = xy_of(b3)
+    pieces = [b0, x_of(b1), y_of(b2), p3]
+
+    scratch = [pltpu.VMEM((blocks, half, span), BF16)]
+    out = call(route_kernel, [slab] * blocks, pieces, scratch, blocks=blocks)
+    got = [out[0]] + [z_of(out[k], k) for k in range(1, blocks)]
+    mine, theirs, *pre = call(
+        tower_kernel,
+        [((half, width), BF16)] * 2 + [((part, units), BF16)] * blocks,
+        got + [tower],
+        [pltpu.VMEM((half, units), F32)],
+        blocks=blocks,
+    )
+    got = [pre[0]] + [z_of(pre[k], k) for k in range(1, blocks)]
+    recv = r_of(theirs)
+    mixed = pl.pallas_call(
+        functools.partial(mixed_kernel, part=part),
+        out_shape=jax.ShapeDtypeStruct((width, tok), BF16),
+        in_specs=[VMEM] * 2,
+        out_specs=VMEM,
+        scratch_shapes=[pltpu.VMEM((tok, width), BF16)],
+        compiler_params=SMALL,
+        name="mixed",
+    )(*[pltpu.with_memory_space_constraint(v, pltpu.VMEM) for v in (mine, recv)])
+    scores = pl.pallas_call(
+        functools.partial(head_kernel, blocks=blocks),
+        out_shape=jax.ShapeDtypeStruct((tower_out.shape[0], part), F32),
+        in_specs=[VMEM] * (blocks + 2) + [SMEM],
+        out_specs=VMEM,
+        compiler_params=SMALL,
+        name="head",
+    )(
+        *[pltpu.with_memory_space_constraint(v, pltpu.VMEM) for v in got + [tower_bias, tower_out]],
+        out_bias.reshape(1, -1),
+    )
+    return (mixed.T, scores)
+
+
 def solution(mesh):
+    groups, n_tensor, n_rep = (mesh.shape[a] for a in ALL)
+
+    def per_device(*args):
+        requests, w_up = args[0], args[3]
+        rows = 2 * groups * requests.shape[0]
+        fits = groups == n_tensor and groups == 2 * 2 and n_rep == 2 and w_up.shape[0] <= 256
+        fits = fits and requests.shape[0] == LANES
+        if fits and rows <= requests.shape[1] * n_tensor * n_rep:
+            return stationary(*args)
+        return moved_weights(*args)
+
     in_specs = (
         P("expert", ("tensor", "rep")),
         P("expert", None),

time: 199 us -> 82 us (0.41)
  blocking collectives: 95.8 us -> 0 us
  starting transfers between devices: 3.68 us -> 37.8 us
  waiting for transfers between devices: 65.8 us -> 31.7 us
  between operations: 14.2 us -> 0.86 us
  matrix products: 7.42 us -> 0 us
  Pallas kernels: 0 us -> 7.26 us
  local copies, waits for them, and re-layouts: 8.73 us -> 3.84 us
  other arithmetic: 2.92 us -> 0.27 us
    all_to_all x3 -> x0, blocking collectives: 79.4 us -> none  [the longest x1 30.1 us: per_device(): lax.all_to_all(w_up, 'expert', split_axis=0, concat_axis=1, tiled=True)]
    ppermute x0 -> x32, starting transfers between devices: none -> 37.8 us  [permute(): return lax.ppermute(x, ALL, pairs)]
    unnamed x3 -> x0, waiting for transfers between devices: 32.7 us -> none
    ppermute x0 -> x32, waiting for transfers between devices: none -> 31.7 us  [permute(): return lax.ppermute(x, ALL, pairs)]
    reduce_scatter x1 -> x0, waiting for transfers between devices: 27.9 us -> none  [per_device(): lax.psum_scatter(jnp.dot(mixed, tower_in, preferred_element_type=jnp.floa...]
    all_gather x1 -> x0, blocking collectives: 16.4 us -> none  [per_device(): full_rows = lax.all_gather(requests, ('tensor', 'rep'), axis=1, tiled=True)]
    dot_general x5 -> x0, matrix products: 7.42 us -> none  [the longest x1 5.47 us: per_device(): jnp.einsum('sech,edh->secd', hidden, serve_down, preferred_element_type=j...]
    pallas_call x0 -> x12, Pallas kernels: none -> 7.26 us  [the longest x10 5.27 us: call(): pl.pallas_call(functools.partial(kernel, **static), out_shape=[pltpu.VMEM...]
  transfers between devices with their start and end apart: 3 -> 32, of which waited for: 3 -> 16; matrix products, arithmetic and copies ran while one was open for 0% -> 0% of each run, Pallas kernels for 0% -> 5%
where the time goes in v2:
time: 82 us; the launch traced here: 81.7 us
  starting transfers between devices  37.8 us (46%)
  waiting for transfers between devices  31.7 us (39%)
  Pallas kernels  7.26 us (9%)
  local copies, waits for them, and re-layouts  3.84 us (5%)
  between operations  0.86 us (1%)
    ppermute x32, starting transfers between devices, permute(): return lax.ppermute(x, ALL, pairs)  37.8 us
    ppermute x32, waiting for transfers between devices, permute(): return lax.ppermute(x, ALL, pairs)  31.7 us
    pallas_call x10, Pallas kernels, call(): pl.pallas_call(functools.partial(kernel, **static), out_shape=[pltpu.VMEM...  5.27 us
    unnamed x18, local copies, waits for them, and re-layouts  3.84 us
  transfers between devices with their start and end apart: 32, of which 16 were waited for; matrix products, arithmetic and copies ran while one was open for 0% of the time, Pallas kernels for 5%

profile of v2, /device:TPU:0, one launch (start us, length us, event | category | flops | bytes accessed | tf_op | source)
XLA Modules:
  0.0 81.7 jit_solution(9077242715134663039)
XLA Ops:
  2.8 5.1 %collective-permute-start.3 = (bf16[208,128]{1,0:T(8,128)(2,1)S(1)}, bf16[208,128]{1,0:T(8,128)(2,1)S(1)}, u32[]{:S(2)}, u32[]{:S(2)}) collective-permute-start(bf16[208,128]{1,0:T(8,128)(2,1)S(1)} %shard_map.104), channel_id=1, source_target_pairs={{0,6},{1,7},{2,14},{3,15},{4,22},{5,23},{6,30},{7,31},{8,4},{9,5},... | collective-permute-start | bytes 159752 | tf_op jit(solution)/shard_map/ppermute | solution.py:85
  7.9 1.5 %collective-permute-start.2 = (bf16[208,128]{1,0:T(8,128)(2,1)S(1)}, bf16[208,128]{1,0:T(8,128)(2,1)S(1)}, u32[]{:S(2)}, u32[]{:S(2)}) collective-permute-start(bf16[208,128]{1,0:T(8,128)(2,1)S(1)} %shard_map.104), channel_id=1, source_target_pairs={{0,4},{1,5},{2,12},{3,13},{4,20},{5,21},{6,28},{7,29},{8,6},{9,7},... | collective-permute-start | bytes 159752 | tf_op jit(solution)/shard_map/ppermute | solution.py:85
  10.7 1.4 %collective-permute-done.2.refs_2_ = bf16[208,128]{1,0:T(8,128)(2,1)S(1)} collective-permute-done((bf16[208,128]{1,0:T(8,128)(2,1)S(1)}, bf16[208,128]{1,0:T(8,128)(2,1)S(1)}, u32[]{:S(2)}, u32[]{:S(2)}) %collective-permute-start.2) | collective-permute-done | bytes 53280 | tf_op jit(solution)/shard_map/ppermute | solution.py:85
  12.1 2.2 %collective-permute-done.1.refs_1_ = bf16[208,128]{1,0:T(8,128)(2,1)S(1)} collective-permute-done((bf16[208,128]{1,0:T(8,128)(2,1)S(1)}, bf16[208,128]{1,0:T(8,128)(2,1)S(1)}, u32[]{:S(2)}, u32[]{:S(2)}) %collective-permute-start.1) | collective-permute-done | bytes 53280 | tf_op jit(solution)/shard_map/ppermute | solution.py:85
  14.7 1.7 %copy-done = bf16[4,384,768]{2,1,0:T(8,128)(2,1)S(1)} copy-done((bf16[4,384,768]{2,1,0:T(8,128)(2,1)S(1)}, bf16[4,384,768]{2,1,0:T(8,128)(2,1)}, u32[]{:S(2)}) %copy-start) | copy-done | bytes 2359320
  17.3 5.2 %collective-permute-start.9 = (bf16[128,768]{1,0:T(8,128)(2,1)S(1)}, bf16[128,768]{1,0:T(8,128)(2,1)S(1)}, u32[]{:S(2)}, u32[]{:S(2)}) collective-permute-start(bf16[128,768]{1,0:T(8,128)(2,1)S(1)} %get-tuple-element.31), channel_id=1, source_target_pairs={{0,8},{1,9},{2,10},{3,11},{4,12},{5,13},{6,14},{7,15},{8,0},{9,1},... | collective-permute-start | bytes 589832 | tf_op jit(solution)/shard_map/ppermute | solution.py:85
  22.5 2.1 %collective-permute-start.15 = (bf16[128,768]{1,0:T(8,128)(2,1)S(1)}, bf16[128,768]{1,0:T(8,128)(2,1)S(1)}, u32[]{:S(2)}, u32[]{:S(2)}) collective-permute-start(bf16[128,768]{1,0:T(8,128)(2,1)S(1)} %get-tuple-element.35), channel_id=1, source_target_pairs={{0,16},{1,17},{2,18},{3,19},{4,20},{5,21},{6,22},{7,23},{8,24},{9,... | collective-permute-start | bytes 589832 | tf_op jit(solution)/shard_map/ppermute | solution.py:85
  24.6 1.6 %shard_map.106 = (bf16[128,768]{1,0:T(8,128)(2,1)S(1)}, bf16[128,768]{1,0:T(8,128)(2,1)S(1)}, bf16[128,768]{1,0:T(8,128)(2,1)S(1)}, bf16[128,768]{1,0:T(8,128)(2...) custom-call(bf16[208,128]{1,0:T(8,128)(2,1)S(1)} %collective-permute-done.refs_0_, ...), custom_call_target="tpu_custom_call" | custom-call | tf_op jit(solution)/shard_map/pallas_call | solution.py:106
  26.4 1.7 %collective-permute-done.9 = bf16[128,768]{1,0:T(8,128)(2,1)S(1)} collective-permute-done((bf16[128,768]{1,0:T(8,128)(2,1)S(1)}, bf16[128,768]{1,0:T(8,128)(2,1)S(1)}, u32[]{:S(2)}, u32[]{:S(2)}) %collective-permute-start.9) | collective-permute-done | bytes 196640 | tf_op jit(solution)/shard_map/ppermute | solution.py:85
  28.2 2.3 %collective-permute-start.10 = (bf16[128,768]{1,0:T(8,128)(2,1)S(1)}, bf16[128,768]{1,0:T(8,128)(2,1)S(1)}, u32[]{:S(2)}, u32[]{:S(2)}) collective-permute-start(bf16[128,768]{1,0:T(8,128)(2,1)S(1)} %add_convert_fusion.1), channel_id=1, source_target_pairs={{0,16},{1,17},{2,18},{3,19},{4,20},{5,21},{6,22},{7,23},{8,24},{9,... | collective-permute-start | bytes 589832 | tf_op jit(solution)/shard_map/ppermute | solution.py:85
  30.6 2.1 %collective-permute-start.16 = (bf16[128,768]{1,0:T(8,128)(2,1)S(1)}, bf16[128,768]{1,0:T(8,128)(2,1)S(1)}, u32[]{:S(2)}, u32[]{:S(2)}) collective-permute-start(bf16[128,768]{1,0:T(8,128)(2,1)S(1)} %add_convert_fusion), channel_id=1, source_target_pairs={{0,8},{1,9},{2,10},{3,11},{4,12},{5,13},{6,14},{7,15},{8,0},{9,1},... | collective-permute-start | bytes 589832 | tf_op jit(solution)/shard_map/ppermute | solution.py:85
  33.4 4.9 %collective-permute-done.10 = bf16[128,768]{1,0:T(8,128)(2,1)S(1)} collective-permute-done((bf16[128,768]{1,0:T(8,128)(2,1)S(1)}, bf16[128,768]{1,0:T(8,128)(2,1)S(1)}, u32[]{:S(2)}, u32[]{:S(2)}) %collective-permute-start.10) | collective-permute-done | bytes 196640 | tf_op jit(solution)/shard_map/ppermute | solution.py:85
  38.4 1.8 %collective-permute-start.12 = (bf16[128,768]{1,0:T(8,128)(2,1)S(1)}, bf16[128,768]{1,0:T(8,128)(2,1)S(1)}, u32[]{:S(2)}, u32[]{:S(2)}) collective-permute-start(bf16[128,768]{1,0:T(8,128)(2,1)S(1)} %maximum_convert_fusion.1.refs_1_), channel_id=1, source_target_pairs={{0,16},{1,17},{2,18},{3,19},{4,20},{5,21},{6,22},{7,23},{8,24},{9,... | collective-permute-start | bytes 589832 | tf_op jit(solution)/shard_map/ppermute | solution.py:85
  40.8 1.6 %collective-permute-start.11 = (bf16[128,768]{1,0:T(8,128)(2,1)S(1)}, bf16[128,768]{1,0:T(8,128)(2,1)S(1)}, u32[]{:S(2)}, u32[]{:S(2)}) collective-permute-start(bf16[128,768]{1,0:T(8,128)(2,1)S(1)} %maximum_convert_fusion.1.refs_1_), channel_id=1, source_target_pairs={{0,8},{1,9},{2,10},{3,11},{4,12},{5,13},{6,14},{7,15},{8,0},{9,1},... | collective-permute-start | bytes 589832 | tf_op jit(solution)/shard_map/ppermute | solution.py:85
  42.7 2.2 %collective-permute-done.12.refs_3_ = bf16[128,768]{1,0:T(8,128)(2,1)S(1)} collective-permute-done((bf16[128,768]{1,0:T(8,128)(2,1)S(1)}, bf16[128,768]{1,0:T(8,128)(2,1)S(1)}, u32[]{:S(2)}, u32[]{:S(2)}) %collective-permute-start.12) | collective-permute-done | bytes 196640 | tf_op jit(solution)/shard_map/ppermute | solution.py:85
  45.4 2.7 %collective-permute-done.17.refs_6_ = bf16[128,768]{1,0:T(8,128)(2,1)S(1)} collective-permute-done((bf16[128,768]{1,0:T(8,128)(2,1)S(1)}, bf16[128,768]{1,0:T(8,128)(2,1)S(1)}, u32[]{:S(2)}, u32[]{:S(2)}) %collective-permute-start.17) | collective-permute-done | bytes 196640 | tf_op jit(solution)/shard_map/ppermute | solution.py:85
  48.7 3.7 %collective-permute-done.11.refs_2_ = bf16[128,768]{1,0:T(8,128)(2,1)S(1)} collective-permute-done((bf16[128,768]{1,0:T(8,128)(2,1)S(1)}, bf16[128,768]{1,0:T(8,128)(2,1)S(1)}, u32[]{:S(2)}, u32[]{:S(2)}) %collective-permute-start.11) | collective-permute-done | bytes 196640 | tf_op jit(solution)/shard_map/ppermute | solution.py:85
  52.4 2.3 %collective-permute-done.13.refs_4_ = bf16[128,768]{1,0:T(8,128)(2,1)S(1)} collective-permute-done((bf16[128,768]{1,0:T(8,128)(2,1)S(1)}, bf16[128,768]{1,0:T(8,128)(2,1)S(1)}, u32[]{:S(2)}, u32[]{:S(2)}) %collective-permute-start.13) | collective-permute-done | bytes 196640 | tf_op jit(solution)/shard_map/ppermute | solution.py:85
  58.5 2.5 %collective-permute-start.24 = (bf16[64,384]{1,0:T(8,128)(2,1)S(1)}, bf16[64,384]{1,0:T(8,128)(2,1)S(1)}, u32[]{:S(2)}, u32[]{:S(2)}) collective-permute-start(bf16[64,384]{1,0:T(8,128)(2,1)S(1)} %get-tuple-element.40), channel_id=1, source_target_pairs={{0,24},{1,25},{2,26},{3,27},{4,28},{5,29},{6,30},{7,31},{8,16},{9,... | collective-permute-start | bytes 147464 | tf_op jit(solution)/shard_map/ppermute | solution.py:85
  63.6 3.5 %collective-permute-start.26 = (bf16[64,384]{1,0:T(8,128)(2,1)S(1)}, bf16[64,384]{1,0:T(8,128)(2,1)S(1)}, u32[]{:S(2)}, u32[]{:S(2)}) collective-permute-start(bf16[64,384]{1,0:T(8,128)(2,1)S(1)} %get-tuple-element.43), channel_id=1, source_target_pairs={{0,4},{1,5},{2,6},{3,7},{4,0},{5,1},{6,2},{7,3},{8,12},{9,13},{10,... | collective-permute-start | bytes 147464 | tf_op jit(solution)/shard_map/ppermute | solution.py:85
  69.2 3.8 %collective-permute-done.27.refs_3_ = bf16[64,384]{1,0:T(8,128)(2,1)S(1)} collective-permute-done((bf16[64,384]{1,0:T(8,128)(2,1)S(1)}, bf16[64,384]{1,0:T(8,128)(2,1)S(1)}, u32[]{:S(2)}, u32[]{:S(2)}) %collective-permute-start.27) | collective-permute-done | bytes 49184 | tf_op jit(solution)/shard_map/ppermute | solution.py:85
  73.4 1.4 %collective-permute-start.30 = (bf16[16,768]{1,0:T(8,128)(2,1)S(1)}, bf16[16,768]{1,0:T(8,128)(2,1)S(1)}, u32[]{:S(2)}, u32[]{:S(2)}) collective-permute-start(bf16[16,768]{1,0:T(8,128)(2,1)S(1)} %get-tuple-element.50), channel_id=1, source_target_pairs={{0,4},{1,5},{2,6},{3,7},{4,0},{5,1},{6,2},{7,3},{8,12},{9,13},{10,... | collective-permute-start | bytes 73736 | tf_op jit(solution)/shard_map/ppermute | solution.py:85
  74.8 3.0 %collective-permute-start.31 = (bf16[16,768]{1,0:T(8,128)(2,1)S(1)}, bf16[16,768]{1,0:T(8,128)(2,1)S(1)}, u32[]{:S(2)}, u32[]{:S(2)}) collective-permute-start(bf16[16,768]{1,0:T(8,128)(2,1)S(1)} %get-tuple-element.51), channel_id=1, source_target_pairs={{0,6},{1,7},{2,4},{3,5},{4,2},{5,3},{6,0},{7,1},{8,14},{9,15},{10,... | collective-permute-start | bytes 73736 | tf_op jit(solution)/shard_map/ppermute | solution.py:85
  78.5 2.0 %collective-permute-done.31.refs_3_ = bf16[16,768]{1,0:T(8,128)(2,1)S(1)} collective-permute-done((bf16[16,768]{1,0:T(8,128)(2,1)S(1)}, bf16[16,768]{1,0:T(8,128)(2,1)S(1)}, u32[]{:S(2)}, u32[]{:S(2)}) %collective-permute-start.31) | collective-permute-done | bytes 24608 | tf_op jit(solution)/shard_map/ppermute | solution.py:85
  (74 shorter events, 18.5 us)
Async XLA Ops:
  2.8 7.8 %collective-permute-start.3 = (bf16[208,128]{1,0:T(8,128)(2,1)S(1)}, bf16[208,128]{1,0:T(8,128)(2,1)S(1)}, u32[]{:S(2)}, u32[]{:S(2)}) collective-permute-start(bf16[208,128]{1,0:T(8,128)(2,1)S(1)} %shard_map.104), channel_id=1, source_target_pairs={{0,6},{1,7},{2,14},{3,15},{4,22},{5,23},{6,30},{7,31},{8,4},{9,5},... | collective-permute-start | bytes 159752 | tf_op jit(solution)/shard_map/ppermute | solution.py:85
  9.5 4.8 %collective-permute-start.1 = (bf16[208,128]{1,0:T(8,128)(2,1)S(1)}, bf16[208,128]{1,0:T(8,128)(2,1)S(1)}, u32[]{:S(2)}, u32[]{:S(2)}) collective-permute-start(bf16[208,128]{1,0:T(8,128)(2,1)S(1)} %shard_map.104), channel_id=1, source_target_pairs={{0,2},{1,3},{2,10},{3,11},{4,18},{5,19},{6,26},{7,27},{8,0},{9,1},... | collective-permute-start | bytes 159752 | tf_op jit(solution)/shard_map/ppermute | solution.py:85
  10.6 6.0 %collective-permute-start.7 = (bf16[208,128]{1,0:T(8,128)(2,1)S(1)}, bf16[208,128]{1,0:T(8,128)(2,1)S(1)}, u32[]{:S(2)}, u32[]{:S(2)}) collective-permute-start(bf16[208,128]{1,0:T(8,128)(2,1)S(1)} %collective-permute-done.3.refs_3_), channel_id=1, source_target_pairs={{0,1},{1,0},{2,3},{3,2},{4,5},{5,4},{6,7},{7,6},{8,9},{9,8},{10,11... | collective-permute-start | bytes 159752 | tf_op jit(solution)/shard_map/ppermute | solution.py:85
  17.3 10.8 %collective-permute-start.9 = (bf16[128,768]{1,0:T(8,128)(2,1)S(1)}, bf16[128,768]{1,0:T(8,128)(2,1)S(1)}, u32[]{:S(2)}, u32[]{:S(2)}) collective-permute-start(bf16[128,768]{1,0:T(8,128)(2,1)S(1)} %get-tuple-element.31), channel_id=1, source_target_pairs={{0,8},{1,9},{2,10},{3,11},{4,12},{5,13},{6,14},{7,15},{8,0},{9,1},... | collective-permute-start | bytes 589832 | tf_op jit(solution)/shard_map/ppermute | solution.py:85
  22.5 8.0 %collective-permute-start.15 = (bf16[128,768]{1,0:T(8,128)(2,1)S(1)}, bf16[128,768]{1,0:T(8,128)(2,1)S(1)}, u32[]{:S(2)}, u32[]{:S(2)}) collective-permute-start(bf16[128,768]{1,0:T(8,128)(2,1)S(1)} %get-tuple-element.35), channel_id=1, source_target_pairs={{0,16},{1,17},{2,18},{3,19},{4,20},{5,21},{6,22},{7,23},{8,24},{9,... | collective-permute-start | bytes 589832 | tf_op jit(solution)/shard_map/ppermute | solution.py:85
  26.2 7.2 %collective-permute-start.8 = (bf16[128,768]{1,0:T(8,128)(2,1)S(1)}, bf16[128,768]{1,0:T(8,128)(2,1)S(1)}, u32[]{:S(2)}, u32[]{:S(2)}) collective-permute-start(bf16[128,768]{1,0:T(8,128)(2,1)S(1)} %get-tuple-element.29), channel_id=1, source_target_pairs={{0,8},{1,9},{2,10},{3,11},{4,12},{5,13},{6,14},{7,15},{8,0},{9,1},... | collective-permute-start | bytes 589832 | tf_op jit(solution)/shard_map/ppermute | solution.py:85
  26.4 13.8 %collective-permute-start.14 = (bf16[128,768]{1,0:T(8,128)(2,1)S(1)}, bf16[128,768]{1,0:T(8,128)(2,1)S(1)}, u32[]{:S(2)}, u32[]{:S(2)}) collective-permute-start(bf16[128,768]{1,0:T(8,128)(2,1)S(1)} %get-tuple-element.33), channel_id=1, source_target_pairs={{0,16},{1,17},{2,18},{3,19},{4,20},{5,21},{6,22},{7,23},{8,24},{9,... | collective-permute-start | bytes 589832 | tf_op jit(solution)/shard_map/ppermute | solution.py:85
  28.2 10.2 %collective-permute-start.10 = (bf16[128,768]{1,0:T(8,128)(2,1)S(1)}, bf16[128,768]{1,0:T(8,128)(2,1)S(1)}, u32[]{:S(2)}, u32[]{:S(2)}) collective-permute-start(bf16[128,768]{1,0:T(8,128)(2,1)S(1)} %add_convert_fusion.1), channel_id=1, source_target_pairs={{0,16},{1,17},{2,18},{3,19},{4,20},{5,21},{6,22},{7,23},{8,24},{9,... | collective-permute-start | bytes 589832 | tf_op jit(solution)/shard_map/ppermute | solution.py:85
  30.6 9.7 %collective-permute-start.16 = (bf16[128,768]{1,0:T(8,128)(2,1)S(1)}, bf16[128,768]{1,0:T(8,128)(2,1)S(1)}, u32[]{:S(2)}, u32[]{:S(2)}) collective-permute-start(bf16[128,768]{1,0:T(8,128)(2,1)S(1)} %add_convert_fusion), channel_id=1, source_target_pairs={{0,8},{1,9},{2,10},{3,11},{4,12},{5,13},{6,14},{7,15},{8,0},{9,1},... | collective-permute-start | bytes 589832 | tf_op jit(solution)/shard_map/ppermute | solution.py:85
  38.4 6.5 %collective-permute-start.12 = (bf16[128,768]{1,0:T(8,128)(2,1)S(1)}, bf16[128,768]{1,0:T(8,128)(2,1)S(1)}, u32[]{:S(2)}, u32[]{:S(2)}) collective-permute-start(bf16[128,768]{1,0:T(8,128)(2,1)S(1)} %maximum_convert_fusion.1.refs_1_), channel_id=1, source_target_pairs={{0,16},{1,17},{2,18},{3,19},{4,20},{5,21},{6,22},{7,23},{8,24},{9,... | collective-permute-start | bytes 589832 | tf_op jit(solution)/shard_map/ppermute | solution.py:85
  40.3 7.8 %collective-permute-start.17 = (bf16[128,768]{1,0:T(8,128)(2,1)S(1)}, bf16[128,768]{1,0:T(8,128)(2,1)S(1)}, u32[]{:S(2)}, u32[]{:S(2)}) collective-permute-start(bf16[128,768]{1,0:T(8,128)(2,1)S(1)} %maximum_convert_fusion.refs_5_), channel_id=1, source_target_pairs={{0,8},{1,9},{2,10},{3,11},{4,12},{5,13},{6,14},{7,15},{8,0},{9,1},... | collective-permute-start | bytes 589832 | tf_op jit(solution)/shard_map/ppermute | solution.py:85
  40.8 7.7 %collective-permute-start.20 = (bf16[192,768]{1,0:T(8,128)(2,1)S(1)}, bf16[192,768]{1,0:T(8,128)(2,1)S(1)}, u32[]{:S(2)}, u32[]{:S(2)}) collective-permute-start(bf16[192,768]{1,0:T(8,128)(2,1)S(1)} %copy-done.2), channel_id=1, source_target_pairs={{0,1},{1,0},{2,3},{3,2},{4,5},{5,4},{6,7},{7,6},{8,9},{9,8},{10,11... | collective-permute-start | bytes 884744 | tf_op jit(solution)/shard_map/ppermute | solution.py:85
  40.8 11.6 %collective-permute-start.11 = (bf16[128,768]{1,0:T(8,128)(2,1)S(1)}, bf16[128,768]{1,0:T(8,128)(2,1)S(1)}, u32[]{:S(2)}, u32[]{:S(2)}) collective-permute-start(bf16[128,768]{1,0:T(8,128)(2,1)S(1)} %maximum_convert_fusion.1.refs_1_), channel_id=1, source_target_pairs={{0,8},{1,9},{2,10},{3,11},{4,12},{5,13},{6,14},{7,15},{8,0},{9,1},... | collective-permute-start | bytes 589832 | tf_op jit(solution)/shard_map/ppermute | solution.py:85
  42.4 10.0 %collective-permute-start.18 = (bf16[128,768]{1,0:T(8,128)(2,1)S(1)}, bf16[128,768]{1,0:T(8,128)(2,1)S(1)}, u32[]{:S(2)}, u32[]{:S(2)}) collective-permute-start(bf16[128,768]{1,0:T(8,128)(2,1)S(1)} %maximum_convert_fusion.refs_5_), channel_id=1, source_target_pairs={{0,16},{1,17},{2,18},{3,19},{4,20},{5,21},{6,22},{7,23},{8,24},{9,... | collective-permute-start | bytes 589832 | tf_op jit(solution)/shard_map/ppermute | solution.py:85
  44.9 9.8 %collective-permute-start.13 = (bf16[128,768]{1,0:T(8,128)(2,1)S(1)}, bf16[128,768]{1,0:T(8,128)(2,1)S(1)}, u32[]{:S(2)}, u32[]{:S(2)}) collective-permute-start(bf16[128,768]{1,0:T(8,128)(2,1)S(1)} %collective-permute-done.12.refs_3_), channel_id=1, source_target_pairs={{0,8},{1,9},{2,10},{3,11},{4,12},{5,13},{6,14},{7,15},{8,0},{9,1},... | collective-permute-start | bytes 589832 | tf_op jit(solution)/shard_map/ppermute | solution.py:85
  48.2 6.5 %collective-permute-start.19 = (bf16[128,768]{1,0:T(8,128)(2,1)S(1)}, bf16[128,768]{1,0:T(8,128)(2,1)S(1)}, u32[]{:S(2)}, u32[]{:S(2)}) collective-permute-start(bf16[128,768]{1,0:T(8,128)(2,1)S(1)} %collective-permute-done.17.refs_6_), channel_id=1, source_target_pairs={{0,16},{1,17},{2,18},{3,19},{4,20},{5,21},{6,22},{7,23},{8,24},{9,... | collective-permute-start | bytes 589832 | tf_op jit(solution)/shard_map/ppermute | solution.py:85
  58.2 4.5 %collective-permute-start.23 = (bf16[64,384]{1,0:T(8,128)(2,1)S(1)}, bf16[64,384]{1,0:T(8,128)(2,1)S(1)}, u32[]{:S(2)}, u32[]{:S(2)}) collective-permute-start(bf16[64,384]{1,0:T(8,128)(2,1)S(1)} %get-tuple-element.39), channel_id=1, source_target_pairs={{0,16},{1,17},{2,18},{3,19},{4,20},{5,21},{6,22},{7,23},{8,24},{9,... | collective-permute-start | bytes 147464 | tf_op jit(solution)/shard_map/ppermute | solution.py:85
  58.5 5.0 %collective-permute-start.24 = (bf16[64,384]{1,0:T(8,128)(2,1)S(1)}, bf16[64,384]{1,0:T(8,128)(2,1)S(1)}, u32[]{:S(2)}, u32[]{:S(2)}) collective-permute-start(bf16[64,384]{1,0:T(8,128)(2,1)S(1)} %get-tuple-element.40), channel_id=1, source_target_pairs={{0,24},{1,25},{2,26},{3,27},{4,28},{5,29},{6,30},{7,31},{8,16},{9,... | collective-permute-start | bytes 147464 | tf_op jit(solution)/shard_map/ppermute | solution.py:85
  63.6 5.6 %collective-permute-start.26 = (bf16[64,384]{1,0:T(8,128)(2,1)S(1)}, bf16[64,384]{1,0:T(8,128)(2,1)S(1)}, u32[]{:S(2)}, u32[]{:S(2)}) collective-permute-start(bf16[64,384]{1,0:T(8,128)(2,1)S(1)} %get-tuple-element.43), channel_id=1, source_target_pairs={{0,4},{1,5},{2,6},{3,7},{4,0},{5,1},{6,2},{7,3},{8,12},{9,13},{10,... | collective-permute-start | bytes 147464 | tf_op jit(solution)/shard_map/ppermute | solution.py:85
  67.1 5.9 %collective-permute-start.27 = (bf16[64,384]{1,0:T(8,128)(2,1)S(1)}, bf16[64,384]{1,0:T(8,128)(2,1)S(1)}, u32[]{:S(2)}, u32[]{:S(2)}) collective-permute-start(bf16[64,384]{1,0:T(8,128)(2,1)S(1)} %get-tuple-element.44), channel_id=1, source_target_pairs={{0,6},{1,7},{2,4},{3,5},{4,2},{5,3},{6,0},{7,1},{8,14},{9,15},{10,... | collective-permute-start | bytes 147464 | tf_op jit(solution)/shard_map/ppermute | solution.py:85
  73.2 4.5 %collective-permute-start.28 = (bf16[64,192]{1,0:T(8,128)(2,1)S(1)}, bf16[64,192]{1,0:T(8,128)(2,1)S(1)}, u32[]{:S(2)}, u32[]{:S(2)}) collective-permute-start(bf16[64,192]{1,0:T(8,128)(2,1)S(1)} %get-tuple-element.47), channel_id=1, source_target_pairs={{0,1},{1,0},{2,3},{3,2},{4,5},{5,4},{6,7},{7,6},{8,9},{9,8},{10,11... | collective-permute-start | bytes 73736 | tf_op jit(solution)/shard_map/ppermute | solution.py:85
  73.3 5.2 %collective-permute-start.29 = (bf16[16,768]{1,0:T(8,128)(2,1)S(1)}, bf16[16,768]{1,0:T(8,128)(2,1)S(1)}, u32[]{:S(2)}, u32[]{:S(2)}) collective-permute-start(bf16[16,768]{1,0:T(8,128)(2,1)S(1)} %get-tuple-element.49), channel_id=1, source_target_pairs={{0,2},{1,3},{2,0},{3,1},{4,6},{5,7},{6,4},{7,5},{8,10},{9,11},{10,... | collective-permute-start | bytes 73736 | tf_op jit(solution)/shard_map/ppermute | solution.py:85
  73.4 5.1 %collective-permute-start.30 = (bf16[16,768]{1,0:T(8,128)(2,1)S(1)}, bf16[16,768]{1,0:T(8,128)(2,1)S(1)}, u32[]{:S(2)}, u32[]{:S(2)}) collective-permute-start(bf16[16,768]{1,0:T(8,128)(2,1)S(1)} %get-tuple-element.50), channel_id=1, source_target_pairs={{0,4},{1,5},{2,6},{3,7},{4,0},{5,1},{6,2},{7,3},{8,12},{9,13},{10,... | collective-permute-start | bytes 73736 | tf_op jit(solution)/shard_map/ppermute | solution.py:85
  74.8 5.6 %collective-permute-start.31 = (bf16[16,768]{1,0:T(8,128)(2,1)S(1)}, bf16[16,768]{1,0:T(8,128)(2,1)S(1)}, u32[]{:S(2)}, u32[]{:S(2)}) collective-permute-start(bf16[16,768]{1,0:T(8,128)(2,1)S(1)} %get-tuple-element.51), channel_id=1, source_target_pairs={{0,6},{1,7},{2,4},{3,5},{4,2},{5,3},{6,0},{7,1},{8,14},{9,15},{10,... | collective-permute-start | bytes 73736 | tf_op jit(solution)/shard_map/ppermute | solution.py:85
  (17 other events, 149.6 us)
